TPU v7x, 128 devices: a whole 4x4x4 slice. The times are simulated.
128 devices in a mesh: flow: 16 (over y, x_hi, core), cross: 8 (over x_lo, z).
Axes of the slice: x: 4 (x_hi: 2, x_lo: 2; x = x_hi * 2 + x_lo), y: 4, z: 4, core: 2. Of those that a mesh axis runs over, the one named last changes fastest.
Arguments:
- solid_temp: float32 [8, 4096, 4096], P(None, 'flow', 'cross'), may hold values from 0.5 to 1.5
- conductance: float32 [8, 4096, 4096], P(None, 'flow', 'cross'), may hold values from 0.03 to 0.12
- coolant: float32 [4, 4096, 4096], P(None, 'flow', 'cross'), may hold values from 0 to 1
- power_index: int32 [4096, 4096], P('flow', 'cross'), may hold values from 0 to 15
- power_levels: float32 [16], replicated, may hold values from 0.05 to 0.5
- channel_mask: int32 [4, 4096], P(None, 'cross'), may hold values 0 or 1
- inlet: float32 [4, 4096], P(None, 'cross'), may hold values from 0 to 0.5
- flow_gain: float32 [4, 4096], P(None, 'cross'), may hold values from 2 to 16
Outputs:
- solid_next: float32 [8, 4096, 4096], P(None, 'flow', 'cross')
- coolant_next: float32 [4, 4096, 4096], P(None, 'flow', 'cross')
All inputs are finite; a program needn't handle non-finite values. No bound on the sum of `channel_mask` on one device may be relied on, other than what follows from the above.
Results may differ from a plain program's by a relative error of at most 0.000058.
Values sent between devices are 32-bit elements; how exact they have to be, the bound alone decides.
No kernel may reach another device: no remote copies, remote signals or barrier semaphores. Data moves between devices by JAX's collectives and lax.ppermute only.
A program may use at most 128 MiB of HBM per device.

v0:
```python
import jax
import jax.numpy as jnp
from jax import lax
from jax.sharding import PartitionSpec as P


def padded_2(shard, sides, width):
    edges = {}
    for axis, dim in sides:
        size, length = (lax.axis_size(axis), shard.shape[dim])
        up = [(i, (i + 1) % size) for i in range(size - 1)]
        last = lax.slice_in_dim(shard, length - width, length, axis=dim)
        initial = lax.slice_in_dim(shard, 0, width, axis=dim)
        edges[dim] = (
            lax.ppermute(last, axis, up),
            lax.ppermute(initial, axis, [(b, a) for a, b in up]),
        )
    done = []
    for _, dim in sides:
        low, high = edges[dim]
        around = [(width, width) if d in done else (0, 0) for d in range(shard.ndim)]
        shard = jnp.concatenate([jnp.pad(low, around), shard, jnp.pad(high, around)], axis=dim)
        done.append(dim)
    return shard


def from_everyone(shard, axis):
    length = lax.axis_size(axis)
    return lax.all_to_all(
        jnp.broadcast_to(shard[None], (length, *shard.shape)), axis, 0, 0, tiled=True
    )


def laid_out(tiles, dim):
    lengths = list(tiles.shape[1:])
    lengths[dim] *= tiles.shape[0]
    return jnp.moveaxis(tiles, 0, dim).reshape(lengths)


def gather_directly(shard, axis, dim):
    tiles = from_everyone(shard, axis)
    return laid_out(tiles, dim)


def advance(padded, conduct, heating, coolant_now, open_cols):
    center = padded[:, 1:-1, 1:-1]
    lateral = (
        padded[:, 2:, 1:-1] + padded[:, :-2, 1:-1] + padded[:, 1:-1, 2:] + padded[:, 1:-1, :-2]
    )
    upward = center[1:] - center[:-1]
    no_layer = jnp.zeros_like(center[:1])
    vertical = jnp.concatenate([upward, no_layer], axis=0) - jnp.concatenate(
        [no_layer, upward], axis=0
    )
    chans = coolant_now.shape[0]
    paired = center.reshape(chans, 2, center.shape[1], center.shape[2])
    film_term = 0.08 * open_cols[:, None, None, :] * (coolant_now[:, None] - paired)
    source = jnp.concatenate([heating[None], jnp.zeros_like(center[1:])], axis=0)
    return (
        center
        + conduct * (lateral - 4.0 * center)
        + 0.05 * vertical
        + film_term.reshape(center.shape)
        + source
    )


def lookup_heat(power_index, power_levels):
    level_ids = jnp.arange(power_levels.shape[0], dtype=jnp.int32)
    matches = (power_index[None] == level_ids[:, None, None]).astype(jnp.float32)
    return jnp.sum(matches * power_levels[:, None, None], axis=0)


def shards(
    solid_temp, conductance, coolant, power_index, power_levels, channel_mask, inlet, flow_gain
):
    chans = coolant.shape[0]
    rows_dev = solid_temp.shape[1]
    cols_dev = solid_temp.shape[2]
    heating = lookup_heat(power_index, power_levels)
    open_cols = channel_mask.astype(jnp.float32)
    current = solid_temp
    for repeat in range(2):
        padded = padded_2(current, (("flow", 1), ("cross", 2)), 1)
        current = advance(padded, conductance, heating, coolant, open_cols)
    paired = current.reshape(chans, 2, rows_dev, cols_dev)
    absorbed = 0.08 * open_cols[:, None, :] * (paired[:, 0] + paired[:, 1] - 2.0 * coolant)
    row_pos = jnp.arange(rows_dev, dtype=jnp.int32)[:, None]
    col_pos = jnp.arange(rows_dev, dtype=jnp.int32)[None, :]
    triangle = jnp.where(col_pos < row_pos, 1.0, jnp.where(col_pos == row_pos, 0.5, 0.0)).astype(
        jnp.float32
    )
    within = jnp.einsum("ij,kjy->kiy", triangle, absorbed, precision=lax.Precision.HIGHEST)
    totals = jnp.sum(absorbed, axis=1)
    everyone = gather_directly(totals[None], "flow", 0)
    weights = (jnp.arange(everyone.shape[0], dtype=jnp.int32) < lax.axis_index("flow")).astype(
        jnp.float32
    )
    carried = jnp.sum(everyone * weights[:, None, None], axis=0)
    length_cells = float(rows_dev * lax.axis_size("flow"))
    fluid_new = (
        inlet[:, None, :] + flow_gain[:, None, :] * (carried[:, None, :] + within) / length_cells
    )
    return (current, fluid_new)


def solution(mesh):
    return jax.shard_map(
        shards,
        mesh=mesh,
        in_specs=(
            P(None, "flow", "cross"),
            P(None, "flow", "cross"),
            P(None, "flow", "cross"),
            P("flow", "cross"),
            P(),
            P(None, "cross"),
            P(None, "cross"),
            P(None, "cross"),
        ),
        out_specs=(P(None, "flow", "cross"), P(None, "flow", "cross")),
        check_vma=False,
    )
```

profile of v0, /device:TPU:3, one launch (start us, length us, event | category | flops | bytes accessed | tf_op | source)
XLA Modules:
  0.0 114.9 jit_solution(317823086081319255)
XLA Ops:
  0.6 1.9 %fusion.40 = (f32[8,256,1]{2,1,0:T(8,128)S(1)}, f32[8,256,1]{2,1,0:T(8,128)S(1)}) fusion(f32[8,256,512]{2,1,0:T(8,128)} %param.8), kind=kLoop, calls=%fused_computation.73 | loop fusion | bytes 32768 | tf_op jit(solution)/shard_map/slice | solution.py:13
  2.5 0.3 copy.74
  2.9 5.6 %collective-permute-start.2 = (f32[8,256,1]{1,0,2:T(8,128)S(1)}, f32[8,256,1]{1,0,2:T(8,128)S(1)}, u32[]{:S(2)}, u32[]{:S(2)}) collective-permute-start(f32[8,256,1]{1,0,2:T(8,128)S(1)} %copy.74), channel_id=1, source_target_pairs={{1,0},{2,1},{3,2},{4,3},{5,4},{6,5},{7,6},{9,8},{10,9},{11,10},{12... | collective-permute-start | bytes 24584 | tf_op jit(solution)/shard_map/ppermute | solution.py:16
  8.5 0.3 copy.75
  8.8 1.9 %collective-permute-start.3 = (f32[8,256,1]{1,0,2:T(8,128)S(1)}, f32[8,256,1]{1,0,2:T(8,128)S(1)}, u32[]{:S(2)}, u32[]{:S(2)}) collective-permute-start(f32[8,256,1]{1,0,2:T(8,128)S(1)} %copy.75), channel_id=1, source_target_pairs={{0,1},{1,2},{2,3},{3,4},{4,5},{5,6},{6,7},{8,9},{9,10},{10,11},{11... | collective-permute-start | bytes 24584 | tf_op jit(solution)/shard_map/ppermute | solution.py:15
  10.8 1.0 fusion.41
  11.8 2.9 %collective-permute-start = (f32[8,1,512]{2,1,0:T(1,128)S(1)}, f32[8,1,512]{2,1,0:T(1,128)S(1)}, u32[]{:S(2)}, u32[]{:S(2)}) collective-permute-start(f32[8,1,512]{2,1,0:T(1,128)S(1)} %get-tuple-element.21), channel_id=1, source_target_pairs={{8,0},{16,8},{24,16},{32,24},{40,32},{48,40},{56,48},{64,56},{72,6... | collective-permute-start | bytes 49160 | tf_op jit(solution)/shard_map/ppermute | solution.py:16
  14.6 0.0 copy-start.3
  14.6 0.0 copy-start.7
  14.7 0.0 copy-start.6
  14.7 4.3 %collective-permute-start.1 = (f32[8,1,512]{2,1,0:T(1,128)S(1)}, f32[8,1,512]{2,1,0:T(1,128)S(1)}, u32[]{:S(2)}, u32[]{:S(2)}) collective-permute-start(f32[8,1,512]{2,1,0:T(1,128)S(1)} %get-tuple-element.20), channel_id=1, source_target_pairs={{0,8},{8,16},{16,24},{24,32},{32,40},{40,48},{48,56},{56,64},{64,7... | collective-permute-start | bytes 49160 | tf_op jit(solution)/shard_map/ppermute | solution.py:15
  19.0 5.9 %slice_subtract_fusion.1 = f32[7,256,512]{2,1,0:T(8,128)} fusion(f32[8,256,512]{2,1,0:T(8,128)} %param.8), kind=kLoop, calls=%fused_computation.47 | loop fusion | flops 917504 | bytes 11010048 | tf_op jit(solution)/shard_map/sub | solution.py:50
  24.9 0.9 select_reduce_fusion
  25.9 0.0 collective-permute-done.2
  25.9 1.4 %copy.60 = f32[8,256,1]{2,1,0:T(8,128)} copy(f32[8,256,1]{1,0,2:T(8,128)S(1)} %collective-permute-done.2) | data formatting | bytes 16384 | tf_op jit(solution)/shard_map/ppermute | solution.py:16
  27.2 0.0 collective-permute-done.3
  27.2 1.3 %copy.62 = f32[8,256,1]{2,1,0:T(8,128)} copy(f32[8,256,1]{1,0,2:T(8,128)S(1)} %collective-permute-done.3) | data formatting | bytes 16384 | tf_op jit(solution)/shard_map/ppermute | solution.py:15
  28.6 0.0 collective-permute-done
  28.6 0.0 collective-permute-done.1
  28.6 15.2 %pad_add_fusion.1 = f32[8,256,512]{2,1,0:T(8,128)S(1)} fusion(f32[1,256,512]{2,1,0:T(8,128)S(1)} %bitcast.51, f32[8,256,512]{2,1,0:T(8,128)} %param.8, f32[8,256,512]{2,1,0:T(8,128)} %param.9, f32[8,256,1]{2,1,0:T(8,128)} %copy.62, f32[8,1,512]{2,1,0:T(1,128)S(1)} %collective-permute-done, f32[8,1,512]{2,1,0:T(1,128)S(1)} %collective-permute-done.1, ...), kind=kLoop, calls=%fused_computation.5 | loop fusion | flops 29360128 | bytes 18939904 | tf_op jit(solution)/shard_map/add | solution.py:60
  43.8 0.0 copy-start
  43.8 1.9 %fusion.38 = (f32[8,256,1]{2,1,0:T(8,128)}, f32[8,256,1]{2,1,0:T(8,128)}) fusion(f32[8,256,512]{2,1,0:T(8,128)S(1)} %pad_add_fusion.1), kind=kLoop, calls=%fused_computation.71 | loop fusion | bytes 32768 | tf_op jit(solution)/shard_map/slice | solution.py:13
  45.7 0.7 copy-done
  46.5 1.5 %copy.63 = f32[8,256,1]{1,0,2:T(8,128)S(1)} copy(f32[8,256,1]{2,1,0:T(8,128)} %get-tuple-element.14) | data formatting | bytes 16384 | tf_op jit(solution)/shard_map/slice | solution.py:13
  48.0 6.1 %collective-permute-start.6 = (f32[8,256,1]{1,0,2:T(8,128)S(1)}, f32[8,256,1]{1,0,2:T(8,128)S(1)}, u32[]{:S(2)}, u32[]{:S(2)}) collective-permute-start(f32[8,256,1]{1,0,2:T(8,128)S(1)} %copy.63), channel_id=1, source_target_pairs={{1,0},{2,1},{3,2},{4,3},{5,4},{6,5},{7,6},{9,8},{10,9},{11,10},{12... | collective-permute-start | bytes 24584 | tf_op jit(solution)/shard_map/ppermute | solution.py:16
  54.1 1.5 %copy.65 = f32[8,256,1]{1,0,2:T(8,128)S(1)} copy(f32[8,256,1]{2,1,0:T(8,128)} %get-tuple-element.15) | data formatting | bytes 16384 | tf_op jit(solution)/shard_map/slice | solution.py:12
  55.7 1.9 %collective-permute-start.7 = (f32[8,256,1]{1,0,2:T(8,128)S(1)}, f32[8,256,1]{1,0,2:T(8,128)S(1)}, u32[]{:S(2)}, u32[]{:S(2)}) collective-permute-start(f32[8,256,1]{1,0,2:T(8,128)S(1)} %copy.65), channel_id=1, source_target_pairs={{0,1},{1,2},{2,3},{3,4},{4,5},{5,6},{6,7},{8,9},{9,10},{10,11},{11... | collective-permute-start | bytes 24584 | tf_op jit(solution)/shard_map/ppermute | solution.py:15
  57.6 1.9 %collective-permute-start.4 = (f32[8,1,512]{2,1,0:T(1,128)S(1)}, f32[8,1,512]{2,1,0:T(1,128)S(1)}, u32[]{:S(2)}, u32[]{:S(2)}) collective-permute-start(f32[8,1,512]{2,1,0:T(1,128)S(1)} %get-tuple-element.17), channel_id=1, source_target_pairs={{8,0},{16,8},{24,16},{32,24},{40,32},{48,40},{56,48},{64,56},{72,6... | collective-permute-start | bytes 49160 | tf_op jit(solution)/shard_map/ppermute | solution.py:16
  59.5 5.3 %collective-permute-start.5 = (f32[8,1,512]{2,1,0:T(1,128)S(1)}, f32[8,1,512]{2,1,0:T(1,128)S(1)}, u32[]{:S(2)}, u32[]{:S(2)}) collective-permute-start(f32[8,1,512]{2,1,0:T(1,128)S(1)} %get-tuple-element.16), channel_id=1, source_target_pairs={{0,8},{8,16},{16,24},{24,32},{32,40},{40,48},{48,56},{56,64},{64,7... | collective-permute-start | bytes 49160 | tf_op jit(solution)/shard_map/ppermute | solution.py:15
  64.9 5.8 %slice_subtract_fusion = f32[7,256,512]{2,1,0:T(8,128)} fusion(f32[8,256,512]{2,1,0:T(8,128)} %copy-done), kind=kLoop, calls=%fused_computation.46 | loop fusion | flops 917504 | bytes 11010048 | tf_op jit(solution)/shard_map/sub | solution.py:50
  70.7 0.0 collective-permute-done.6
  70.7 1.4 %copy.64 = f32[8,256,1]{2,1,0:T(8,128)} copy(f32[8,256,1]{1,0,2:T(8,128)S(1)} %collective-permute-done.6) | data formatting | bytes 16384 | tf_op jit(solution)/shard_map/ppermute | solution.py:16
  72.1 0.0 collective-permute-done.7
  72.1 1.3 %copy.66 = f32[8,256,1]{2,1,0:T(8,128)} copy(f32[8,256,1]{1,0,2:T(8,128)S(1)} %collective-permute-done.7) | data formatting | bytes 16384 | tf_op jit(solution)/shard_map/ppermute | solution.py:15
  73.4 0.0 collective-permute-done.4
  73.4 0.0 collective-permute-done.5
  73.4 15.5 %pad_add_fusion = f32[8,256,512]{2,1,0:T(8,128)S(1)} fusion(f32[1,256,512]{2,1,0:T(8,128)S(1)} %bitcast.52, f32[8,256,512]{2,1,0:T(8,128)} %copy-done, f32[8,256,512]{2,1,0:T(8,128)} %param.9, f32[8,256,1]{2,1,0:T(8,128)} %copy.66, f32[8,1,512]{2,1,0:T(1,128)S(1)} %collective-permute-done.4, f32[8,1,512]{2,1,0:T(1,128)S(1)} %collective-permute-done.5, ...), kind=kLoop, calls=%fused_computation.4 | loop fusion | flops 29360128 | bytes 18939904 | tf_op jit(solution)/shard_map/add | solution.py:60
  88.9 0.0 copy-start.2
  88.9 0.0 copy-start.4
  88.9 0.0 copy-start.5
  88.9 2.5 %fusion.36 = (f32[4,512]{1,0:T(4,128)S(1)}, f32[4,256,512]{2,1,0:T(8,128)}) fusion(f32[4,256,512]{2,1,0:T(8,128)S(1)} %copy-done.1, f32[4,2,256,512]{3,2,1,0:T(8,128)S(1)} %bitcast.50, f32[4,512]{1,0:T(4,128)S(1)} %convert_multiply_fusion), kind=kLoop, calls=%fused_computation.70 | loop fusion | flops 2619392 | bytes 8404992 | tf_op jit(solution)/shard_map/reduce_sum | solution.py:94
  91.4 0.1 copy-done.2
  91.5 0.7 broadcast_in_dim.16
  92.2 7.6 %all-to-all-start = ((f32[16,1,4,512]{3,2,1,0:T(4,128)}), f32[16,1,4,512]{3,2,1,0:T(4,128)S(1)}, u32[]{:S(2)}, u32[]{:S(2)}) async-start(f32[16,1,4,512]{3,2,1,0:T(4,128)} %broadcast_in_dim.16), calls=%async_computation | async-start | bytes 262144 | tf_op jit(solution)/shard_map/all_to_all | solution.py:29
  99.8 7.6 %all-to-all-done = f32[16,1,4,512]{3,2,1,0:T(4,128)S(1)} async-done(((f32[16,1,4,512]{3,2,1,0:T(4,128)}), f32[16,1,4,512]{3,2,1,0:T(4,128)S(1)}, u32[]{:S(2)}, u32[]{:S(2)}) %all-to-all-start) | async-done | bytes 131104 | tf_op jit(solution)/shard_map/all_to_all | solution.py:29
  107.4 0.1 fusion.29
  107.6 5.5 %add_bitcast_fusion = f32[4,256,512]{1,2,0:T(8,128)S(1)} fusion(f32[4,256,512]{2,1,0:T(8,128)} %get-tuple-element.13, f32[4,512]{1,0:T(4,128)S(1)} %fusion.29, f32[4,512]{1,0:T(4,128)S(1)} %copy-done.4, f32[4,512]{1,0:T(4,128)S(1)} %copy-done.5), kind=kOutput, calls=%fused_computation.54 | convolution fusion | flops 1612972032 | bytes 4218880 | tf_op jit(solution)/shard_map/ij,kjy->kiy/dot_general | solution.py:93
  113.0 1.8 %copy.71 = f32[4,256,512]{2,1,0:T(8,128)} copy(f32[4,256,512]{1,2,0:T(8,128)S(1)} %add_bitcast_fusion) | data formatting | bytes 4194304
  (12 shorter events, 0.1 us)
Async XLA Ops:
  2.9 23.0 %collective-permute-start.2 = (f32[8,256,1]{1,0,2:T(8,128)S(1)}, f32[8,256,1]{1,0,2:T(8,128)S(1)}, u32[]{:S(2)}, u32[]{:S(2)}) collective-permute-start(f32[8,256,1]{1,0,2:T(8,128)S(1)} %copy.74), channel_id=1, source_target_pairs={{1,0},{2,1},{3,2},{4,3},{5,4},{6,5},{7,6},{9,8},{10,9},{11,10},{12... | collective-permute-start | bytes 24584 | tf_op jit(solution)/shard_map/ppermute | solution.py:16
  8.8 18.4 %collective-permute-start.3 = (f32[8,256,1]{1,0,2:T(8,128)S(1)}, f32[8,256,1]{1,0,2:T(8,128)S(1)}, u32[]{:S(2)}, u32[]{:S(2)}) collective-permute-start(f32[8,256,1]{1,0,2:T(8,128)S(1)} %copy.75), channel_id=1, source_target_pairs={{0,1},{1,2},{2,3},{3,4},{4,5},{5,6},{6,7},{8,9},{9,10},{10,11},{11... | collective-permute-start | bytes 24584 | tf_op jit(solution)/shard_map/ppermute | solution.py:15
  11.8 16.8 %collective-permute-start = (f32[8,1,512]{2,1,0:T(1,128)S(1)}, f32[8,1,512]{2,1,0:T(1,128)S(1)}, u32[]{:S(2)}, u32[]{:S(2)}) collective-permute-start(f32[8,1,512]{2,1,0:T(1,128)S(1)} %get-tuple-element.21), channel_id=1, source_target_pairs={{8,0},{16,8},{24,16},{32,24},{40,32},{48,40},{56,48},{64,56},{72,6... | collective-permute-start | bytes 49160 | tf_op jit(solution)/shard_map/ppermute | solution.py:16
  14.6 10.3 %copy-start.3 = (s32[256,512]{1,0:T(8,128)S(1)}, s32[256,512]{1,0:T(8,128)}, u32[]{:S(2)}) copy-start(s32[256,512]{1,0:T(8,128)} %param.11) | copy-start | bytes 1572868
  14.6 10.2 %copy-start.7 = (f32[16]{0:T(128)S(1)}, f32[16]{0:T(128)}, u32[]{:S(2)}) copy-start(f32[16]{0:T(128)} %param.12) | copy-start | bytes 196
  14.7 11.1 %copy-start.6 = (s32[4,512]{1,0:T(4,128)S(1)}, s32[4,512]{1,0:T(4,128)}, u32[]{:S(2)}) copy-start(s32[4,512]{1,0:T(4,128)} %param.13) | copy-start | bytes 24580
  14.7 13.9 %collective-permute-start.1 = (f32[8,1,512]{2,1,0:T(1,128)S(1)}, f32[8,1,512]{2,1,0:T(1,128)S(1)}, u32[]{:S(2)}, u32[]{:S(2)}) collective-permute-start(f32[8,1,512]{2,1,0:T(1,128)S(1)} %get-tuple-element.20), channel_id=1, source_target_pairs={{0,8},{8,16},{16,24},{24,32},{32,40},{40,48},{48,56},{56,64},{64,7... | collective-permute-start | bytes 49160 | tf_op jit(solution)/shard_map/ppermute | solution.py:15
  24.9 3.7 %copy-start.1 = (f32[4,256,512]{2,1,0:T(8,128)S(1)}, f32[4,256,512]{2,1,0:T(8,128)}, u32[]{:S(2)}) copy-start(f32[4,256,512]{2,1,0:T(8,128)} %param.10) | copy-start | bytes 6291460
  43.8 2.6 %copy-start = (f32[8,256,512]{2,1,0:T(8,128)}, f32[8,256,512]{2,1,0:T(8,128)S(1)}, u32[]{:S(2)}) copy-start(f32[8,256,512]{2,1,0:T(8,128)S(1)} %pad_add_fusion.1) | copy-start | bytes 12582916
  48.0 22.7 %collective-permute-start.6 = (f32[8,256,1]{1,0,2:T(8,128)S(1)}, f32[8,256,1]{1,0,2:T(8,128)S(1)}, u32[]{:S(2)}, u32[]{:S(2)}) collective-permute-start(f32[8,256,1]{1,0,2:T(8,128)S(1)} %copy.63), channel_id=1, source_target_pairs={{1,0},{2,1},{3,2},{4,3},{5,4},{6,5},{7,6},{9,8},{10,9},{11,10},{12... | collective-permute-start | bytes 24584 | tf_op jit(solution)/shard_map/ppermute | solution.py:16
  55.7 16.4 %collective-permute-start.7 = (f32[8,256,1]{1,0,2:T(8,128)S(1)}, f32[8,256,1]{1,0,2:T(8,128)S(1)}, u32[]{:S(2)}, u32[]{:S(2)}) collective-permute-start(f32[8,256,1]{1,0,2:T(8,128)S(1)} %copy.65), channel_id=1, source_target_pairs={{0,1},{1,2},{2,3},{3,4},{4,5},{5,6},{6,7},{8,9},{9,10},{10,11},{11... | collective-permute-start | bytes 24584 | tf_op jit(solution)/shard_map/ppermute | solution.py:15
  57.6 15.8 %collective-permute-start.4 = (f32[8,1,512]{2,1,0:T(1,128)S(1)}, f32[8,1,512]{2,1,0:T(1,128)S(1)}, u32[]{:S(2)}, u32[]{:S(2)}) collective-permute-start(f32[8,1,512]{2,1,0:T(1,128)S(1)} %get-tuple-element.17), channel_id=1, source_target_pairs={{8,0},{16,8},{24,16},{32,24},{40,32},{48,40},{56,48},{64,56},{72,6... | collective-permute-start | bytes 49160 | tf_op jit(solution)/shard_map/ppermute | solution.py:16
  59.5 13.9 %collective-permute-start.5 = (f32[8,1,512]{2,1,0:T(1,128)S(1)}, f32[8,1,512]{2,1,0:T(1,128)S(1)}, u32[]{:S(2)}, u32[]{:S(2)}) collective-permute-start(f32[8,1,512]{2,1,0:T(1,128)S(1)} %get-tuple-element.16), channel_id=1, source_target_pairs={{0,8},{8,16},{16,24},{24,32},{32,40},{40,48},{48,56},{56,64},{64,7... | collective-permute-start | bytes 49160 | tf_op jit(solution)/shard_map/ppermute | solution.py:15
  88.9 2.6 %copy-start.2 = (f32[8,256,512]{2,1,0:T(8,128)}, f32[8,256,512]{2,1,0:T(8,128)S(1)}, u32[]{:S(2)}) copy-start(f32[8,256,512]{2,1,0:T(8,128)S(1)} %pad_add_fusion) | copy-start | bytes 12582916
  88.9 18.6 %copy-start.4 = (f32[4,512]{1,0:T(4,128)S(1)}, f32[4,512]{1,0:T(4,128)}, u32[]{:S(2)}) copy-start(f32[4,512]{1,0:T(4,128)} %param.15) | copy-start | bytes 24580
  88.9 18.6 %copy-start.5 = (f32[4,512]{1,0:T(4,128)S(1)}, f32[4,512]{1,0:T(4,128)}, u32[]{:S(2)}) copy-start(f32[4,512]{1,0:T(4,128)} %param.14) | copy-start | bytes 24580
  92.2 15.2 %all-to-all-start = ((f32[16,1,4,512]{3,2,1,0:T(4,128)}), f32[16,1,4,512]{3,2,1,0:T(4,128)S(1)}, u32[]{:S(2)}, u32[]{:S(2)}) async-start(f32[16,1,4,512]{3,2,1,0:T(4,128)} %broadcast_in_dim.16), calls=%async_computation | async-start | bytes 262144 | tf_op jit(solution)/shard_map/all_to_all | solution.py:29
where the time goes:
time: 116 us; the launch traced here: 115 us
  other arithmetic  45.9 us (40%)
  starting transfers between devices  37.6 us (32%)
  local copies, waits for them, and re-layouts  17.3 us (15%)
  waiting for transfers between devices  7.63 us (7%)
  matrix products  5.48 us (5%)
    add x2, other arithmetic, advance(): center + conduct * (lateral - 4.0 * center) + 0.05 * vertical  30.6 us
    ppermute x4, starting transfers between devices, padded_2(): lax.ppermute(initial, axis, [(b, a) for a, b in up])  16.5 us
    ppermute x4, starting transfers between devices, padded_2(): lax.ppermute(last, axis, up)  13.5 us
    sub x2, other arithmetic, advance(): upward = center[1:] - center[:-1]  11.7 us
    all_to_all x1, starting transfers between devices, from_everyone(): lax.all_to_all(jnp.broadcast_to(shard[None], (length, *shard.shape)), axi...  7.62 us
    all_to_all x1, waiting for transfers between devices, from_everyone(): lax.all_to_all(jnp.broadcast_to(shard[None], (length, *shard.shape)), axi...  7.61 us
    dot_general x1, matrix products, shards(): jnp.einsum('ij,kjy->kiy', triangle, absorbed, precision=lax.Precision.HIG...  5.48 us
    slice x3, local copies, waits for them, and re-layouts, padded_2(): initial = lax.slice_in_dim(shard, 0, width, axis=dim)  5.4 us
  transfers between devices with their start and end apart: 9, of which 1 were waited for; matrix products, arithmetic and copies ran while one was open for 18% of the time, Pallas kernels for 0%

commit v1 on v0

v1 whole, which is shorter than its diff:
```python
import functools

import jax
import jax.numpy as jnp
from jax import lax
from jax.experimental import pallas as pl
from jax.experimental.pallas import tpu as pltpu
from jax.sharding import PartitionSpec as P

LANES = 128
SUB = 8
VERTICAL = 0.05
FILM = 0.08
VMEM = pl.BlockSpec(memory_space=pltpu.VMEM)
SMEM = pl.BlockSpec(memory_space=pltpu.SMEM)
HBM = pl.BlockSpec(memory_space=pltpu.HBM)


def cut(c):
    return slice(c * LANES, (c + 1) * LANES)


def iota(dim):
    return lax.broadcasted_iota(jnp.int32, (SUB, LANES), dim)


def looked_up(index, levels_ref):
    values = [levels_ref[i] for i in range(levels_ref.shape[0])]
    bit = 0
    while len(values) > 1:
        odd = (index & (1 << bit)) != 0
        values = [jnp.where(odd, b, a) for a, b in zip(values[::2], values[1::2])]
        bit += 1
    return values[0]


def parity(axis):
    return lax.rem(lax.axis_index(axis), 2)


def edge_rows(levels_ref, s_ref, c_ref, w_ref, p_ref, even_ref, odd_ref, s_buf, c_buf, w_buf, p_buf, sems):
    layers, length, _ = s_ref.shape
    chans = w_ref.shape[0]
    copies = []
    for side, at in ((0, 0), (1, length - SUB)):
        for n, (src, dst) in enumerate(((s_ref, s_buf), (c_ref, c_buf), (w_ref, w_buf), (p_ref, p_buf))):
            view = src.at[pl.ds(at, SUB), :] if n == 3 else src.at[:, pl.ds(at, SUB), :]
            copies.append(pltpu.make_async_copy(view, dst.at[side], sems.at[side, n]))
            copies[-1].start()
    for copy in copies:
        copy.wait()

    def fill(out, side, near, far):
        for l in range(layers):
            out[l : l + 1, :] = s_buf[side, l, near : near + 1, :]
            out[layers + l : layers + l + 1, :] = s_buf[side, l, far : far + 1, :]
            out[2 * layers + l : 2 * layers + l + 1, :] = c_buf[side, l, near : near + 1, :]
        for k in range(chans):
            out[3 * layers + k : 3 * layers + k + 1, :] = w_buf[side, k, near : near + 1, :]
        heat = looked_up(p_buf[side, near : near + 1, :], levels_ref)
        for k in range(chans):
            out[3 * layers + chans + k : 3 * layers + chans + k + 1, :] = heat

    par = parity("flow")

    @pl.when(par == 0)
    def _():
        fill(even_ref, 1, 7, 6)
        fill(odd_ref, 0, 0, 1)

    @pl.when(par != 0)
    def _():
        fill(odd_ref, 1, 7, 6)
        fill(even_ref, 0, 0, 1)


def set_film(mask_ref, film):
    for k in range(mask_ref.shape[0]):
        row = mask_ref[k : k + 1, :].astype(jnp.float32) * FILM
        film[k] = jnp.broadcast_to(row, film.shape[1:])


def stencil(l, load, c_ref, w_ref, film, top, bottom, sides, emit, length, layers, tiles):
    row, lane = iota(0), iota(1)
    k = l // 2
    above_l, below_l = jnp.maximum(l - 1, 0), jnp.minimum(l + 1, layers - 1)
    f = [film[k, :, cut(c)] for c in range(tiles)]
    keep = [(1.0 - 2.0 * VERTICAL) - v for v in f]
    count = length // SUB
    down = lambda v: pltpu.roll(v, 1, 0)
    up = lambda v: pltpu.roll(v, SUB - 1, 0)
    if top is None:
        before = [jnp.zeros((SUB, LANES), jnp.float32)] * tiles
        final = before
    else:
        before = [top[l, :, cut(c)] for c in range(tiles)]
        final = None
    u = [load(l, 0, c) for c in range(tiles)]
    u_up = [up(v) for v in u]
    for r in range(count):
        if r + 1 < count:
            after = [load(l, (r + 1) * SUB, c) for c in range(tiles)]
            after_up = [up(v) for v in after]
        elif final is None:
            after = [bottom[l, :, cut(c)] for c in range(tiles)]
            after_up = after
        else:
            after = after_up = final
        u_down = [down(v) for v in u]
        east = [pltpu.roll(v, 1, 1) for v in u]
        west = [pltpu.roll(v, LANES - 1, 1) for v in u]
        left, right = sides(r)
        at = r * SUB
        conds, outs, ws = [], [], []
        for c in range(tiles):
            n = jnp.where(row == 0, before[c], u_down[c])
            s = jnp.where(row == SUB - 1, after_up[c], u_up[c])
            lf = jnp.where(lane == 0, left if c == 0 else east[c - 1], east[c])
            rt = jnp.where(lane == LANES - 1, right if c == tiles - 1 else west[c + 1], west[c])
            cond = c_ref[l, at : at + SUB, cut(c)]
            w = w_ref[k, at : at + SUB, cut(c)]
            around = ((n + s) + (lf + rt)) - 4.0 * u[c]
            beside = load(above_l, at, c) + load(below_l, at, c)
            outs.append((keep[c] * u[c] + cond * around) + (VERTICAL * beside + f[c] * w))
            conds.append(cond)
            ws.append(w)
        emit(r, u, conds, outs, ws)
        before, u, u_up = u_down, after, after_up


def first_step(levels_ref, s_ref, c_ref, w_ref, p_ref, mask_ref, s1_ref, heat_ref, flat_ref, film):
    layers, length, width = s_ref.shape
    tiles = width // LANES
    zero = jnp.zeros((SUB, LANES), jnp.float32)
    set_film(mask_ref, film)

    def layer(l, carry):
        def load(m, at, c):
            return s_ref[m, at : at + SUB, cut(c)]

        def emit(r, u, conds, outs, ws):
            at = r * SUB
            for c in range(tiles):
                s1_ref[l, at : at + SUB, cut(c)] = outs[c]

        stencil(l, load, c_ref, w_ref, film, None, None, lambda r: (zero, zero), emit, length, layers, tiles)
        return carry

    lax.fori_loop(0, layers, layer, 0)
    for r in range(length // SUB):
        at = r * SUB
        for c in range(tiles):
            heat = looked_up(p_ref[at : at + SUB, cut(c)], levels_ref)
            heat_ref[at : at + SUB, cut(c)] = heat
            s1_ref[0, at : at + SUB, cut(c)] += heat
    for n, ref in enumerate((s_ref, c_ref, s1_ref)):
        for l in range(layers):
            for side in range(2):
                turned = ref[l, :, cut(side * (tiles - 1))].T
                j = 64 * side + n * SUB + l
                flat_ref[j : j + 1, :] = turned[0:1, :] if side == 0 else turned[LANES - 1 :, :]


def add_rows(s_ref, c_ref, mask_ref, re_ref, ro_ref, flat_ref, s1_in, s1_ref, halo_ref, even_ref, odd_ref, rows):
    layers, length, width = s_ref.shape
    chans = mask_ref.shape[0]
    tiles = width // LANES
    last = tiles - 1
    row, lane = iota(0), iota(1)
    zero = jnp.zeros((SUB, LANES), jnp.float32)
    fpar, cpar = parity("flow"), parity("cross")
    for l in range(layers):
        rows[0, l : l + 1, :] = s_ref[l, 0:1, :]
        rows[1, l : l + 1, :] = s_ref[l, length - 1 : length, :]
        rows[2, l : l + 1, :] = mask_ref[l // 2 : l // 2 + 1, :].astype(jnp.float32) * FILM

    top = lambda a, b, c: jnp.where(fpar == 0, ro_ref[a:b, cut(c)], re_ref[a:b, cut(c)])
    bottom = lambda a, b, c: jnp.where(fpar == 0, re_ref[a:b, cut(c)], ro_ref[a:b, cut(c)])
    nears = []
    for side, halo in ((0, top), (1, bottom)):
        near = [halo(0, layers, c) for c in range(tiles)]
        nears.append(near)
        east = [pltpu.roll(v, 1, 1) for v in near]
        west = [pltpu.roll(v, LANES - 1, 1) for v in near]
        at = 0 if side == 0 else length - SUB
        for c in range(tiles):
            cond = halo(2 * layers, 3 * layers, c)
            rest = halo(3 * layers, 4 * layers, c)
            heat = jnp.where(row == 0, jnp.broadcast_to(rest[chans : chans + 1, :], (SUB, LANES)), 0.0)
            cool = zero
            for k in range(chans):
                cool = jnp.where(row // 2 == k, jnp.broadcast_to(rest[k : k + 1, :], (SUB, LANES)), cool)
            u = near[c]
            lf = jnp.where(lane == 0, zero if c == 0 else east[c - 1], east[c])
            rt = jnp.where(lane == LANES - 1, zero if c == last else west[c + 1], west[c])
            around = (halo(layers, 2 * layers, c) + rows[side, :, cut(c)]) + (lf + rt)
            over = jnp.where(row == 0, u, pltpu.roll(u, 1, 0))
            under = jnp.where(row == SUB - 1, u, pltpu.roll(u, SUB - 1, 0))
            halo_ref[side * layers : (side + 1) * layers, cut(c)] = (
                u
                + cond * (around - 4.0 * u)
                + VERTICAL * ((over - u) + (under - u))
                + rows[2, :, cut(c)] * (cool - u)
                + heat
            )
            spot = 0 if side == 0 else SUB - 1
            for l in range(layers):
                outside = jnp.broadcast_to(u[l : l + 1, :], (SUB, LANES))
                more = jnp.where(row == spot, c_ref[l, at : at + SUB, cut(c)] * outside, 0.0)
                s1_ref[l, at : at + SUB, cut(c)] = s1_in[l, at : at + SUB, cut(c)] + more

    back = LANES - 1
    def fill(right_ref, left_ref):
        for is_left, out in ((0, right_ref), (1, left_ref)):
            base = 0 if is_left else 64
            tile = 0 if is_left else last
            out[0:16, :] = flat_ref[base : base + 16, :]
            t, b = nears[0][tile], nears[1][tile]
            t0 = t if is_left else pltpu.roll(t, 1, 1)
            b1 = pltpu.roll(b, back, 1) if is_left else b
            out[16:24, 0:LANES] = flat_ref[base + 16 : base + 24, 0:LANES] + jnp.where(
                lane == 0, flat_ref[base + 8 : base + 16, 0:LANES] * t0, 0.0
            )
            out[16:24, LANES:] = flat_ref[base + 16 : base + 24, LANES:] + jnp.where(
                lane == back, flat_ref[base + 8 : base + 16, LANES:] * b1, 0.0
            )
            shift = back if is_left else 1
            out[24:32, 0:LANES] = pltpu.roll(t, shift, 1)
            out[24:32, LANES:] = pltpu.roll(b, shift, 1)

    @pl.when(cpar == 0)
    def _():
        fill(even_ref, odd_ref)

    @pl.when(cpar != 0)
    def _():
        fill(odd_ref, even_ref)


def second_step(
    s1_ref, c_ref, w_ref, heat_ref, mask_ref, re_ref, ro_ref, halo_ref, own_ref, ce_ref, co_ref,
    s2_ref, absorbed_out, total_ref, film, top, bottom, edge, columns, sums_ref, out_buf, absorbed_ref, sem, absorbed_sem,
):
    layers, length, width = s1_ref.shape
    chans = w_ref.shape[0]
    tiles = width // LANES
    last_tile = tiles - 1
    lane = iota(1)
    fpar, cpar = parity("flow"), parity("cross")
    set_film(mask_ref, film)
    got_left = jnp.where(cpar == 0, co_ref[...], ce_ref[...])
    got_right = jnp.where(cpar == 0, ce_ref[...], co_ref[...])
    row = iota(0)
    middle = jnp.zeros((LANES - 2 * SUB, LANES), jnp.float32)
    beyond = (
        (got_left[0:8, :], got_right[0:8, :]),
        (
            got_left[16:24, :] + got_left[8:16, :] * own_ref[0:8, :],
            got_right[16:24, :] + got_right[8:16, :] * own_ref[64:72, :],
        ),
    )
    for n, (lefts, rights) in enumerate(beyond):
        for l in range(layers):
            for half in range(length // LANES):
                first = jnp.where(row == 0, jnp.broadcast_to(lefts[l : l + 1, cut(half)], (SUB, LANES)), 0.0)
                final = jnp.where(row == SUB - 1, jnp.broadcast_to(rights[l : l + 1, cut(half)], (SUB, LANES)), 0.0)
                turned = jnp.concatenate([first, middle, final], axis=0).T
                columns[n, l, half * LANES : (half + 1) * LANES, :] = turned

    cond_top = jnp.where(fpar == 0, ro_ref[16:24, :], re_ref[16:24, :])
    cond_bottom = jnp.where(fpar == 0, re_ref[16:24, :], ro_ref[16:24, :])
    for at, out, cond in ((0, top, cond_top), (1, bottom, cond_bottom)):
        for c in range(tiles):
            value = halo_ref[at * layers : (at + 1) * layers, cut(c)]
            if c == 0:
                value += cond[:, cut(c)] * jnp.where(lane == 0, got_left[24:32, cut(at)], 0.0)
            if c == last_tile:
                value += cond[:, cut(c)] * jnp.where(lane == LANES - 1, got_right[24:32, cut(at)], 0.0)
            for l in range(layers):
                out[l, :, cut(c)] = jnp.broadcast_to(value[l : l + 1, :], (SUB, LANES))

    def complete(l, carry):
        for r in range(length // SUB):
            at = r * SUB
            beside = columns[0, l, at : at + SUB, :]
            for e, c, spot in ((0, 0, 0), (1, last_tile, LANES - 1)):
                more = c_ref[l, at : at + SUB, cut(c)] * jnp.where(lane == spot, beside, 0.0)
                edge[e, l, at : at + SUB, :] = s1_ref[l, at : at + SUB, cut(c)] + more
        return carry

    lax.fori_loop(0, layers, complete, 0)

    def load(m, at, c):
        if c == 0:
            return edge[0, m, at : at + SUB, :]
        if c == last_tile:
            return edge[1, m, at : at + SUB, :]
        return s1_ref[m, at : at + SUB, cut(c)]

    def layer(l, carry):
        def sides(r):
            beside = columns[1, l, r * SUB : (r + 1) * SUB, :]
            return beside, beside

        def emit(r, u, conds, outs, ws):
            at = r * SUB
            for c in range(tiles):
                out = outs[c]
                out_buf[l, at : at + SUB, cut(c)] = out

        stencil(l, load, c_ref, w_ref, film, top, bottom, sides, emit, length, layers, tiles)

        @pl.when(l == 0)
        def _():
            for r in range(length // SUB):
                at = r * SUB
                out_buf[0, at : at + SUB, :] += heat_ref[at : at + SUB, :]

        pltpu.make_async_copy(out_buf.at[l], s2_ref.at[l], sem.at[l]).start()

        @pl.when(lax.rem(l, 2) == 1)
        def _():
            k = l // 2
            for c in range(tiles):
                f = film[k, :, cut(c)]
                total = [jnp.zeros((SUB, LANES), jnp.float32)] * 4
                for r in range(length // SUB):
                    at = r * SUB
                    pair = out_buf[l - 1, at : at + SUB, cut(c)] + out_buf[l, at : at + SUB, cut(c)]
                    value = f * (pair - 2.0 * w_ref[k, at : at + SUB, cut(c)])
                    absorbed_ref[k, at : at + SUB, cut(c)] = value
                    total[r % 4] = total[r % 4] + value
                sums_ref[k, :, cut(c)] = (total[0] + total[1]) + (total[2] + total[3])
            pltpu.make_async_copy(absorbed_ref.at[k], absorbed_out.at[k], absorbed_sem.at[k]).start()

        return carry

    lax.fori_loop(0, layers, layer, 0)
    for k in range(chans):
        row_sum = jnp.sum(sums_ref[k], axis=0, keepdims=True)
        for j in range(total_ref.shape[0]):
            total_ref[j, 0, k : k + 1, :] = row_sum
    for l in range(layers):
        pltpu.make_async_copy(out_buf.at[l], s2_ref.at[l], sem.at[l]).wait()
    for k in range(chans):
        pltpu.make_async_copy(absorbed_ref.at[k], absorbed_out.at[k], absorbed_sem.at[k]).wait()


def march(length_cells, absorbed_ref, inlet_ref, gain_ref, part_ref):
    chans, length, _ = absorbed_ref.shape
    i = lax.broadcasted_iota(jnp.int32, (length, length), 0)
    j = lax.broadcasted_iota(jnp.int32, (length, length), 1)
    triangle = jnp.where(j < i, 1.0, jnp.where(j == i, 0.5, 0.0)).astype(jnp.bfloat16)
    for k in range(chans):
        absorbed = absorbed_ref[k]
        within = None
        for _ in range(3):
            term = absorbed.astype(jnp.bfloat16)
            absorbed = absorbed - term.astype(jnp.float32)
            product = jnp.dot(triangle, term, preferred_element_type=jnp.float32)
            within = product if within is None else within + product
        scale = gain_ref[k : k + 1, :] * (1.0 / length_cells)
        part_ref[k] = inlet_ref[k : k + 1, :] + scale * within


def finish(length_cells, part_ref, every_ref, gain_ref, out_ref, buf, sem):
    flow = lax.axis_index("flow")
    total = jnp.zeros(gain_ref.shape, jnp.float32)
    for j in range(every_ref.shape[0]):
        total += jnp.where(j < flow, every_ref[j, 0], 0.0)
    carried = total * gain_ref[...] * (1.0 / length_cells)
    chans = part_ref.shape[0]
    copies = []
    for k in range(chans):
        buf[k] = part_ref[k] + carried[k : k + 1, :]
        copies.append(pltpu.make_async_copy(buf.at[k], out_ref.at[k], sem.at[k]))
        copies[-1].start()
    for copy in copies:
        copy.wait()


def swaps(size):
    even = [(i, i ^ 1) for i in range(size)]
    odd = [(i, i + 1 if i % 2 else i - 1) for i in range(1, size - 1)]
    return even, odd


def f32(*dims):
    return jax.ShapeDtypeStruct(dims, jnp.float32)


def call(kernel, name, out_shape, in_specs, out_specs, scratch, mib, flops, **kw):
    return pl.pallas_call(
        kernel,
        out_shape=out_shape,
        in_specs=in_specs,
        out_specs=out_specs,
        scratch_shapes=scratch,
        compiler_params=pltpu.CompilerParams(vmem_limit_bytes=int(mib * 2**20)),
        cost_estimate=pl.CostEstimate(flops=int(flops), bytes_accessed=0, transcendentals=0),
        name=name,
        **kw,
    )


def shards(s0, cond, cool, index, levels, mask, inlet, gain):
    layers, length, width = s0.shape
    chans = cool.shape[0]
    flows = lax.axis_size("flow")
    count = 4 * layers
    block = f32(layers, length, width)
    buf = lambda *dims: pltpu.VMEM(dims, jnp.float32)
    hbm = lambda *dims: pltpu.HBM(dims, jnp.float32)
    dma = lambda *dims: pltpu.SemaphoreType.DMA(dims)
    in_hbm = lambda x: pltpu.with_memory_space_constraint(x, pltpu.HBM)
    even, odd = call(
        edge_rows, "edge_rows", (f32(count, width), f32(count, width)), [SMEM] + [HBM] * 4, (VMEM, VMEM),
        [
            buf(2, layers, SUB, width), buf(2, layers, SUB, width), buf(2, chans, SUB, width),
            pltpu.VMEM((2, SUB, width), jnp.int32), dma(2, 4),
        ],
        4, 1e5,
    )(levels, in_hbm(s0), in_hbm(cond), in_hbm(cool), in_hbm(index))
    even_pairs, odd_pairs = swaps(flows)
    row_odd = lax.ppermute(odd, "flow", odd_pairs)
    row_even = lax.ppermute(even, "flow", even_pairs)

    work = 20 * layers * length * width
    s1, heat, own = call(
        first_step, "first_step", (block, f32(length, width), f32(LANES, length)), [SMEM] + [VMEM] * 5, (VMEM,) * 3,
        [buf(chans, SUB, width)], 17, work,
    )(levels, s0, cond, cool, index, mask)
    s1, halo, even, odd = call(
        add_rows, "add_rows", (block, f32(2 * layers, width), f32(32, length), f32(32, length)), [VMEM] * 7, (VMEM,) * 4,
        [buf(3, layers, width)], 17, 1e5, input_output_aliases={6: 0},
    )(s0, cond, mask, row_even, row_odd, own, s1)
    even_pairs, odd_pairs = swaps(lax.axis_size("cross"))
    col_odd = lax.ppermute(odd, "cross", odd_pairs)
    col_even = lax.ppermute(even, "cross", even_pairs)

    s2, absorbed, totals = call(
        second_step, "second_step",
        (hbm(layers, length, width), hbm(chans, length, width), f32(flows, 1, chans, width)),
        [VMEM] * 11, (HBM, HBM, VMEM),
        [
            buf(chans, SUB, width), buf(layers, SUB, width), buf(layers, SUB, width), buf(2, layers, length, LANES),
            buf(2, layers, length, LANES), buf(chans, SUB, width), buf(layers, length, width), buf(chans, length, width), dma(layers), dma(chans),
        ],
        22, work,
    )(s1, cond, cool, heat, mask, row_even, row_odd, halo, own, col_even, col_odd)
    everyone = lax.all_to_all(totals, "flow", 0, 0, tiled=True)

    cells = float(length * flows)
    part = call(
        functools.partial(march, cells), "march", f32(chans, length, width), [VMEM] * 3, VMEM, [], 10, work // 4,
    )(absorbed, inlet, gain)
    fluid = call(
        functools.partial(finish, cells), "finish", hbm(chans, length, width), [VMEM] * 3, HBM,
        [buf(chans, length, width), dma(chans)], 6, 1e5,
    )(part, everyone, gain)
    return s2, fluid


def solution(mesh):
    return jax.shard_map(
        shards,
        mesh=mesh,
        in_specs=(
            P(None, "flow", "cross"),
            P(None, "flow", "cross"),
            P(None, "flow", "cross"),
            P("flow", "cross"),
            P(),
            P(None, "cross"),
            P(None, "cross"),
            P(None, "cross"),
        ),
        out_specs=(P(None, "flow", "cross"), P(None, "flow", "cross")),
        check_vma=False,
    )
```

time: 116 us -> 47 us (0.41)
  other arithmetic: 45.9 us -> 0 us
  starting transfers between devices: 37.6 us -> 18.4 us
  Pallas kernels: 0 us -> 17.7 us
  local copies, waits for them, and re-layouts: 17.3 us -> 3.1 us
  matrix products: 5.48 us -> 0 us
    add x2 -> x0, other arithmetic: 30.6 us -> none  [advance(): center + conduct * (lateral - 4.0 * center) + 0.05 * vertical]
    ppermute x8 -> x4, starting transfers between devices: 30 us -> 11.3 us  [the longest x1 5.01 us: shards(): col_odd = lax.ppermute(odd, 'cross', odd_pairs)]
    pallas_call x0 -> x6, Pallas kernels: none -> 17.7 us  [the longest x1 6.87 us: shards(): call(second_step, 'second_step', (hbm(layers, length, width), hbm(chans,...]
    sub x2 -> x0, other arithmetic: 11.7 us -> none  [advance(): upward = center[1:] - center[:-1]]
    slice x6 -> x0, local copies, waits for them, and re-layouts: 7.97 us -> none  [the longest x3 5.4 us: padded_2(): initial = lax.slice_in_dim(shard, 0, width, axis=dim)]
    dot_general x1 -> x0, matrix products: 5.48 us -> none  [shards(): jnp.einsum('ij,kjy->kiy', triangle, absorbed, precision=lax.Precision.HIG...]
    ppermute x4 -> x0, local copies, waits for them, and re-layouts: 5.41 us -> none  [the longest x2 2.72 us: padded_2(): lax.ppermute(initial, axis, [(b, a) for a, b in up])]
    reduce_sum x3 -> x0, other arithmetic: 3.52 us -> none  [the longest x1 2.53 us: shards(): totals = jnp.sum(absorbed, axis=1)]
  transfers between devices with their start and end apart: 9 -> 5, of which waited for: 1 -> 2; matrix products, arithmetic and copies ran while one was open for 18% -> 0% of each run, Pallas kernels for 0% -> 15%
where the time goes in v1:
time: 47 us; the launch traced here: 46.7 us
  starting transfers between devices  18.4 us (39%)
  Pallas kernels  17.7 us (38%)
  waiting for transfers between devices  6.68 us (14%)
  local copies, waits for them, and re-layouts  3.1 us (7%)
  between operations  0.82 us (2%)
    all_to_all x1, starting transfers between devices, shards(): everyone = lax.all_to_all(totals, 'flow', 0, 0, tiled=True)  7.12 us
    pallas_call x1, Pallas kernels, shards(): call(second_step, 'second_step', (hbm(layers, length, width), hbm(chans,...  6.87 us
    pallas_call x1, Pallas kernels, shards(): call(first_step, 'first_step', (block, f32(length, width), f32(LANES, len...  5.79 us
    ppermute x1, starting transfers between devices, shards(): col_odd = lax.ppermute(odd, 'cross', odd_pairs)  5.01 us
    all_to_all x1, waiting for transfers between devices, shards(): everyone = lax.all_to_all(totals, 'flow', 0, 0, tiled=True)  4.94 us
    ppermute x1, starting transfers between devices, shards(): row_odd = lax.ppermute(odd, 'flow', odd_pairs)  3.78 us
    unnamed x20, local copies, waits for them, and re-layouts  3.1 us
    pallas_call x1, Pallas kernels, shards(): call(edge_rows, 'edge_rows', (f32(count, width), f32(count, width)), [SME...  2.45 us
  transfers between devices with their start and end apart: 5, of which 2 were waited for; matrix products, arithmetic and copies ran while one was open for 0% of the time, Pallas kernels for 15%

profile of v1, /device:TPU:3, one launch (start us, length us, event | category | flops | bytes accessed | tf_op | source)
XLA Modules:
  0.0 46.7 jit_solution(16551411814298028411)
XLA Ops:
  0.6 0.0 copy-start
  0.6 0.0 copy-start.2
  0.7 0.0 copy-start.1
  0.7 0.0 copy-start.3
  0.7 0.0 copy-start.8
  0.7 0.8 %copy-done.8 = f32[16]{0:T(128)S(1)} copy-done((f32[16]{0:T(128)S(1)}, f32[16]{0:T(128)}, u32[]{:S(2)}) %copy-start.8) | copy-done | bytes 88
  1.5 0.0 copy-start.9
  1.5 2.4 %edge_rows.1 = (f32[32,512]{1,0:T(8,128)S(1)}, f32[32,512]{1,0:T(8,128)S(1)}) custom-call(f32[16]{0:T(128)S(1)} %copy-done.8, f32[8,256,512]{2,1,0:T(8,128)} %s_ref.5, f32[8,256,512]{2,1,0:T(8,128)} %c_ref.7, f32[4,256,512]{2,1,0:T(8,128)} %w_ref.5, s32[256,512]{1,0:T(8,128)} %p_ref.3), custom_call_target="tpu_custom_call" | custom-call | flops 100000 | tf_op jit(solution)/shard_map/edge_rows/pallas_call | solution.py:416
  3.9 0.8 %collective-permute-start = (f32[32,512]{1,0:T(8,128)S(1)}, f32[32,512]{1,0:T(8,128)S(1)}, u32[]{:S(2)}, u32[]{:S(2)}) collective-permute-start(f32[32,512]{1,0:T(8,128)S(1)} %get-tuple-element.14), channel_id=1, source_target_pairs={{0,8},{8,0},{16,24},{24,16},{32,40},{40,32},{48,56},{56,48},{64,72... | collective-permute-start | bytes 196616 | tf_op jit(solution)/shard_map/ppermute | solution.py:426
  4.7 3.8 %collective-permute-start.1 = (f32[32,512]{1,0:T(8,128)S(1)}, f32[32,512]{1,0:T(8,128)S(1)}, u32[]{:S(2)}, u32[]{:S(2)}) collective-permute-start(f32[32,512]{1,0:T(8,128)S(1)} %get-tuple-element.15), channel_id=1, source_target_pairs={{8,16},{16,8},{24,32},{32,24},{40,48},{48,40},{56,64},{64,56},{72,... | collective-permute-start | bytes 196616 | tf_op jit(solution)/shard_map/ppermute | solution.py:425
  8.5 0.0 copy-done
  8.5 0.0 copy-done.2
  8.5 0.0 copy-done.1
  8.5 0.0 copy-done.3
  8.5 0.0 copy-done.9
  8.5 0.0 copy-start.5
  8.5 0.7 %copy-done.5 = s32[4,512]{1,0:T(4,128)S(1)} copy-done((s32[4,512]{1,0:T(4,128)S(1)}, s32[4,512]{1,0:T(4,128)}, u32[]{:S(2)}) %copy-start.5) | copy-done | bytes 8216
  9.2 5.8 %first_step.1 = (f32[8,256,512]{2,1,0:T(8,128)S(1)}, f32[256,512]{1,0:T(8,128)S(1)}, f32[128,256]{1,0:T(8,128)S(1)}) custom-call(f32[16]{0:T(128)S(1)} %copy-done.9, f32[8,256,512]{2,1,0:T(8,128)S(1)} %copy-done.1, f32[8,256,512]{2,1,0:T(8,128)S(1)} %copy-done, f32[4,256,512]{2,1,0:T(8,128)S(1)} %copy-done.2, s32[256,512]{1,0:T(8,128)S(1)} %copy-done.3, ...), custom_call_target="tpu_custom_call" | custom-call | flops 20971520 | tf_op jit(solution)/shard_map/first_step/pallas_call | solution.py:429
  15.0 0.0 collective-permute-done.re_ref
  15.0 0.0 collective-permute-done.1.ro_ref
  15.0 0.2 add_rows.1
  15.2 1.7 %collective-permute-start.2 = (f32[32,256]{1,0:T(8,128)S(1)}, f32[32,256]{1,0:T(8,128)S(1)}, u32[]{:S(2)}, u32[]{:S(2)}) collective-permute-start(f32[32,256]{1,0:T(8,128)S(1)} %get-tuple-element.21), channel_id=1, source_target_pairs={{0,1},{1,0},{2,3},{3,2},{4,5},{5,4},{6,7},{7,6},{8,9},{9,8},{10,11... | collective-permute-start | bytes 98312 | tf_op jit(solution)/shard_map/ppermute | solution.py:439
  16.9 5.0 %collective-permute-start.3 = (f32[32,256]{1,0:T(8,128)S(1)}, f32[32,256]{1,0:T(8,128)S(1)}, u32[]{:S(2)}, u32[]{:S(2)}) collective-permute-start(f32[32,256]{1,0:T(8,128)S(1)} %get-tuple-element.22), channel_id=1, source_target_pairs={{1,2},{2,1},{3,4},{4,3},{5,6},{6,5},{9,10},{10,9},{11,12},{12,11},... | collective-permute-start | bytes 98312 | tf_op jit(solution)/shard_map/ppermute | solution.py:438
  21.9 0.0 collective-permute-done.2.ce_ref
  22.0 1.7 %collective-permute-done.3.co_ref = f32[32,256]{1,0:T(8,128)S(1)} collective-permute-done((f32[32,256]{1,0:T(8,128)S(1)}, f32[32,256]{1,0:T(8,128)S(1)}, u32[]{:S(2)}, u32[]{:S(2)}) %collective-permute-start.3) | collective-permute-done | bytes 32800 | tf_op jit(solution)/shard_map/ppermute | solution.py:438
  23.7 0.0 copy-start.6
  23.7 0.0 copy-start.7
  23.7 6.9 %second_step.1 = (f32[8,256,512]{2,1,0:T(8,128)}, f32[4,256,512]{2,1,0:T(8,128)}, f32[16,1,4,512]{3,2,1,0:T(4,128)}) custom-call(f32[8,256,512]{2,1,0:T(8,128)S(1)} %get-tuple-element.18.s1_ref, f32[8,256,512]{2,1,0:T(8,128)S(1)} %copy-done, f32[4,256,512]{2,1,0:T(8,128)S(1)} %copy-done.2, f32[256,512]{1,0:T(8,128)S(1)} %get-tuple-element.19.heat_ref, ...), custom_call_target="tpu_custom_call" | custom-call | flops 20971520 | tf_op jit(solution)/shard_map/second_step/pallas_call | solution.py:441
  30.6 7.1 %all-to-all-start = ((f32[16,1,4,512]{3,2,1,0:T(4,128)}), f32[16,1,4,512]{3,2,1,0:T(4,128)S(1)}, u32[]{:S(2)}, u32[]{:S(2)}) async-start(f32[16,1,4,512]{3,2,1,0:T(4,128)} %get-tuple-element.25), calls=%async_computation | async-start | bytes 262144 | tf_op jit(solution)/shard_map/all_to_all | solution.py:451
  37.7 0.0 copy-done.6
  37.7 0.0 copy-done.7
  37.7 0.0 copy-start.4
  37.7 1.6 %copy-done.4 = f32[4,256,512]{2,1,0:T(8,128)S(1)} copy-done((f32[4,256,512]{2,1,0:T(8,128)S(1)}, f32[4,256,512]{2,1,0:T(8,128)}, u32[]{:S(2)}) %copy-start.4) | copy-done | bytes 2097176
  39.3 1.1 %march.1.part_ref = f32[4,256,512]{2,1,0:T(8,128)S(1)} custom-call(f32[4,256,512]{2,1,0:T(8,128)S(1)} %copy-done.4, f32[4,512]{1,0:T(4,128)S(1)} %copy-done.7, f32[4,512]{1,0:T(4,128)S(1)} %copy-done.6), custom_call_target="tpu_custom_call" | custom-call | flops 5242880 | tf_op jit(solution)/shard_map/march/pallas_call | solution.py:454
  40.4 4.9 %all-to-all-done.every_ref = f32[16,1,4,512]{3,2,1,0:T(4,128)S(1)} async-done(((f32[16,1,4,512]{3,2,1,0:T(4,128)}), f32[16,1,4,512]{3,2,1,0:T(4,128)S(1)}, u32[]{:S(2)}, u32[]{:S(2)}) %all-to-all-start) | async-done | bytes 131104 | tf_op jit(solution)/shard_map/all_to_all | solution.py:451
  45.3 1.4 %finish.1 = f32[4,256,512]{2,1,0:T(8,128)} custom-call(f32[4,256,512]{2,1,0:T(8,128)S(1)} %march.1.part_ref, f32[16,1,4,512]{3,2,1,0:T(4,128)S(1)} %all-to-all-done.every_ref, f32[4,512]{1,0:T(4,128)S(1)} %copy-done.6), custom_call_target="tpu_custom_call" | custom-call | flops 100000 | tf_op jit(solution)/shard_map/finish/pallas_call | solution.py:457
Async XLA Ops:
  0.6 7.9 %copy-start = (f32[8,256,512]{2,1,0:T(8,128)S(1)}, f32[8,256,512]{2,1,0:T(8,128)}, u32[]{:S(2)}) copy-start(f32[8,256,512]{2,1,0:T(8,128)} %c_ref.7) | copy-start | bytes 12582916
  0.6 7.9 %copy-start.2 = (f32[4,256,512]{2,1,0:T(8,128)S(1)}, f32[4,256,512]{2,1,0:T(8,128)}, u32[]{:S(2)}) copy-start(f32[4,256,512]{2,1,0:T(8,128)} %w_ref.5) | copy-start | bytes 6291460
  0.7 7.9 %copy-start.1 = (f32[8,256,512]{2,1,0:T(8,128)S(1)}, f32[8,256,512]{2,1,0:T(8,128)}, u32[]{:S(2)}) copy-start(f32[8,256,512]{2,1,0:T(8,128)} %s_ref.5) | copy-start | bytes 12582916
  0.7 7.9 %copy-start.3 = (s32[256,512]{1,0:T(8,128)S(1)}, s32[256,512]{1,0:T(8,128)}, u32[]{:S(2)}) copy-start(s32[256,512]{1,0:T(8,128)} %p_ref.3) | copy-start | bytes 1572868
  0.7 0.8 %copy-start.8 = (f32[16]{0:T(128)S(1)}, f32[16]{0:T(128)}, u32[]{:S(2)}) copy-start(f32[16]{0:T(128)} %levels_ref.3) | copy-start | bytes 196
  1.5 7.0 %copy-start.9 = (f32[16]{0:T(128)S(1)}, f32[16]{0:T(128)}, u32[]{:S(2)}) copy-start(f32[16]{0:T(128)} %levels_ref.3) | copy-start | bytes 196
  3.9 11.1 %collective-permute-start = (f32[32,512]{1,0:T(8,128)S(1)}, f32[32,512]{1,0:T(8,128)S(1)}, u32[]{:S(2)}, u32[]{:S(2)}) collective-permute-start(f32[32,512]{1,0:T(8,128)S(1)} %get-tuple-element.14), channel_id=1, source_target_pairs={{0,8},{8,0},{16,24},{24,16},{32,40},{40,32},{48,56},{56,48},{64,72... | collective-permute-start | bytes 196616 | tf_op jit(solution)/shard_map/ppermute | solution.py:426
  4.7 10.3 %collective-permute-start.1 = (f32[32,512]{1,0:T(8,128)S(1)}, f32[32,512]{1,0:T(8,128)S(1)}, u32[]{:S(2)}, u32[]{:S(2)}) collective-permute-start(f32[32,512]{1,0:T(8,128)S(1)} %get-tuple-element.15), channel_id=1, source_target_pairs={{8,16},{16,8},{24,32},{32,24},{40,48},{48,40},{56,64},{64,56},{72,... | collective-permute-start | bytes 196616 | tf_op jit(solution)/shard_map/ppermute | solution.py:425
  8.5 0.7 %copy-start.5 = (s32[4,512]{1,0:T(4,128)S(1)}, s32[4,512]{1,0:T(4,128)}, u32[]{:S(2)}) copy-start(s32[4,512]{1,0:T(4,128)} %mask_ref.5) | copy-start | bytes 24580
  15.2 6.7 %collective-permute-start.2 = (f32[32,256]{1,0:T(8,128)S(1)}, f32[32,256]{1,0:T(8,128)S(1)}, u32[]{:S(2)}, u32[]{:S(2)}) collective-permute-start(f32[32,256]{1,0:T(8,128)S(1)} %get-tuple-element.21), channel_id=1, source_target_pairs={{0,1},{1,0},{2,3},{3,2},{4,5},{5,4},{6,7},{7,6},{8,9},{9,8},{10,11... | collective-permute-start | bytes 98312 | tf_op jit(solution)/shard_map/ppermute | solution.py:439
  16.9 6.8 %collective-permute-start.3 = (f32[32,256]{1,0:T(8,128)S(1)}, f32[32,256]{1,0:T(8,128)S(1)}, u32[]{:S(2)}, u32[]{:S(2)}) collective-permute-start(f32[32,256]{1,0:T(8,128)S(1)} %get-tuple-element.22), channel_id=1, source_target_pairs={{1,2},{2,1},{3,4},{4,3},{5,6},{6,5},{9,10},{10,9},{11,12},{12,11},... | collective-permute-start | bytes 98312 | tf_op jit(solution)/shard_map/ppermute | solution.py:438
  23.7 14.0 %copy-start.6 = (f32[4,512]{1,0:T(4,128)S(1)}, f32[4,512]{1,0:T(4,128)}, u32[]{:S(2)}) copy-start(f32[4,512]{1,0:T(4,128)} %gain_ref.3) | copy-start | bytes 24580
  23.7 14.0 %copy-start.7 = (f32[4,512]{1,0:T(4,128)S(1)}, f32[4,512]{1,0:T(4,128)}, u32[]{:S(2)}) copy-start(f32[4,512]{1,0:T(4,128)} %inlet_ref.1) | copy-start | bytes 24580
  30.6 14.7 %all-to-all-start = ((f32[16,1,4,512]{3,2,1,0:T(4,128)}), f32[16,1,4,512]{3,2,1,0:T(4,128)S(1)}, u32[]{:S(2)}, u32[]{:S(2)}) async-start(f32[16,1,4,512]{3,2,1,0:T(4,128)} %get-tuple-element.25), calls=%async_computation | async-start | bytes 262144 | tf_op jit(solution)/shard_map/all_to_all | solution.py:451
  37.7 1.6 %copy-start.4 = (f32[4,256,512]{2,1,0:T(8,128)S(1)}, f32[4,256,512]{2,1,0:T(8,128)}, u32[]{:S(2)}) copy-start(f32[4,256,512]{2,1,0:T(8,128)} %get-tuple-element.24.absorbed_ref) | copy-start | bytes 6291460

commit v2 on v1

v2 whole, which is shorter than its diff:
```python
import functools

import jax
import jax.numpy as jnp
from jax import lax
from jax.experimental import pallas as pl
from jax.experimental.pallas import tpu as pltpu
from jax.sharding import PartitionSpec as P

LANES = 128
SUB = 8
VERTICAL = 0.05
FILM = 0.08
VMEM = pl.BlockSpec(memory_space=pltpu.VMEM)
SMEM = pl.BlockSpec(memory_space=pltpu.SMEM)
HBM = pl.BlockSpec(memory_space=pltpu.HBM)


def cut(c):
    return slice(c * LANES, (c + 1) * LANES)


def iota(dim):
    return lax.broadcasted_iota(jnp.int32, (SUB, LANES), dim)


def looked_up(index, levels_ref):
    values = [levels_ref[i] for i in range(levels_ref.shape[0])]
    bit = 0
    while len(values) > 1:
        odd = (index & (1 << bit)) != 0
        values = [jnp.where(odd, b, a) for a, b in zip(values[::2], values[1::2])]
        bit += 1
    return values[0]


def parity(axis):
    return lax.rem(lax.axis_index(axis), 2)


def edge_rows(
    levels_ref, s_ref, c_ref, w_ref, p_ref, mask_ref, even_ref, odd_ref, film_ref,
    s_buf, c_buf, w_buf, p_buf, mask_buf, levels_buf, sems, more_sems,
):
    layers, length, _ = s_ref.shape
    chans = w_ref.shape[0]
    copies = []
    for side, at in ((0, 0), (1, length - SUB)):
        for n, (src, dst) in enumerate(((s_ref, s_buf), (c_ref, c_buf), (w_ref, w_buf), (p_ref, p_buf))):
            view = src.at[pl.ds(at, SUB), :] if n == 3 else src.at[:, pl.ds(at, SUB), :]
            copies.append(pltpu.make_async_copy(view, dst.at[side], sems.at[side, n]))
    copies.append(pltpu.make_async_copy(mask_ref, mask_buf, more_sems.at[0]))
    copies.append(pltpu.make_async_copy(levels_ref, levels_buf, more_sems.at[1]))
    for copy in copies:
        copy.start()
    for copy in copies:
        copy.wait()
    set_film(mask_buf, film_ref)

    def fill(out, side, near, far):
        for l in range(layers):
            out[l : l + 1, :] = s_buf[side, l, near : near + 1, :]
            out[layers + l : layers + l + 1, :] = s_buf[side, l, far : far + 1, :]
            out[2 * layers + l : 2 * layers + l + 1, :] = c_buf[side, l, near : near + 1, :]
        for k in range(chans):
            out[3 * layers + k : 3 * layers + k + 1, :] = w_buf[side, k, near : near + 1, :]
        heat = looked_up(p_buf[side, near : near + 1, :], levels_buf)
        for k in range(chans):
            out[3 * layers + chans + k : 3 * layers + chans + k + 1, :] = heat

    par = parity("flow")

    @pl.when(par == 0)
    def _():
        fill(even_ref, 1, 7, 6)
        fill(odd_ref, 0, 0, 1)

    @pl.when(par != 0)
    def _():
        fill(odd_ref, 1, 7, 6)
        fill(even_ref, 0, 0, 1)


def set_film(mask_ref, film):
    for k in range(mask_ref.shape[0]):
        row = mask_ref[k : k + 1, :].astype(jnp.float32) * FILM
        film[k] = jnp.broadcast_to(row, film.shape[1:])


def stencil(l, load, c_ref, w_ref, film, a_ref, make, top, bottom, emit, length, layers, tiles):
    row, lane = iota(0), iota(1)
    zero = jnp.zeros((SUB, LANES), jnp.float32)
    k = l // 2
    above_l, below_l = jnp.maximum(l - 1, 0), jnp.minimum(l + 1, layers - 1)
    f = [film[k, :, cut(c)] for c in range(tiles)]
    keep = [(1.0 - 2.0 * VERTICAL) - v for v in f]
    count = length // SUB
    down = lambda v: pltpu.roll(v, 1, 0)
    up = lambda v: pltpu.roll(v, SUB - 1, 0)
    if top is None:
        before = [jnp.zeros((SUB, LANES), jnp.float32)] * tiles
        final = before
    else:
        before = [top[l, :, cut(c)] for c in range(tiles)]
        final = None
    u = [load(l, 0, c) for c in range(tiles)]
    u_up = [up(v) for v in u]
    for r in range(count):
        if r + 1 < count:
            after = [load(l, (r + 1) * SUB, c) for c in range(tiles)]
            after_up = [up(v) for v in after]
        elif final is None:
            after = [bottom[l, :, cut(c)] for c in range(tiles)]
            after_up = after
        else:
            after = after_up = final
        u_down = [down(v) for v in u]
        east = [pltpu.roll(v, 1, 1) for v in u]
        west = [pltpu.roll(v, LANES - 1, 1) for v in u]
        at = r * SUB
        conds, outs, ws = [], [], []
        for c in range(tiles):
            n = jnp.where(row == 0, before[c], u_down[c])
            s = jnp.where(row == SUB - 1, after_up[c], u_up[c])
            lf = jnp.where(lane == 0, zero if c == 0 else east[c - 1], east[c])
            rt = jnp.where(lane == LANES - 1, zero if c == tiles - 1 else west[c + 1], west[c])
            cond = c_ref[l, at : at + SUB, cut(c)]
            w = w_ref[k, at : at + SUB, cut(c)]
            if make:
                own = keep[c] - 4.0 * cond
                a_ref[l, at : at + SUB, cut(c)] = own
            else:
                own = a_ref[l, at : at + SUB, cut(c)]
            beside = load(above_l, at, c) + load(below_l, at, c)
            outs.append((own * u[c] + cond * ((n + s) + (lf + rt))) + (VERTICAL * beside + f[c] * w))
            conds.append(cond)
            ws.append(w)
        emit(r, u, conds, outs, ws)
        before, u, u_up = u_down, after, after_up


def first_step(levels_ref, s_ref, c_ref, w_ref, p_ref, film, s1_ref, a_ref, heat_ref, flat_ref):
    layers, length, width = s_ref.shape
    tiles = width // LANES
    zero = jnp.zeros((SUB, LANES), jnp.float32)

    def layer(l, carry):
        def load(m, at, c):
            return s_ref[m, at : at + SUB, cut(c)]

        def emit(r, u, conds, outs, ws):
            at = r * SUB
            for c in range(tiles):
                s1_ref[l, at : at + SUB, cut(c)] = outs[c]

        stencil(l, load, c_ref, w_ref, film, a_ref, True, None, None, emit, length, layers, tiles)
        return carry

    lax.fori_loop(0, layers, layer, 0)
    table = zero
    for n in range(levels_ref.shape[0]):
        table = jnp.where(iota(1) == n, levels_ref[n], table)
    for r in range(length // SUB):
        at = r * SUB
        for c in range(tiles):
            heat = jnp.take_along_axis(table, p_ref[at : at + SUB, cut(c)], axis=1)
            heat_ref[at : at + SUB, cut(c)] = heat
            s1_ref[0, at : at + SUB, cut(c)] += heat
    lane = lax.broadcasted_iota(jnp.int32, (length, LANES), 1)
    for n, ref in enumerate((s_ref, c_ref, s1_ref)):
        for l in range(layers):
            turned = jnp.where(lane < LANES // 2, ref[l, :, cut(0)], ref[l, :, cut(tiles - 1)]).T
            j = n * SUB + l
            flat_ref[j : j + 1, :] = turned[0:1, :]
            flat_ref[j + 64 : j + 65, :] = turned[LANES - 1 :, :]
            if n == 1:
                flat_ref[j + 16 : j + 17, :] = turned[1:2, :]
                flat_ref[j + 80 : j + 81, :] = turned[LANES - 2 : LANES - 1, :]


def add_rows(s_ref, c_ref, film, re_ref, ro_ref, flat_ref, s1_in, s1_ref, halo_ref, even_ref, odd_ref, rows):
    layers, length, width = s_ref.shape
    chans = film.shape[0]
    tiles = width // LANES
    last = tiles - 1
    row, lane = iota(0), iota(1)
    zero = jnp.zeros((SUB, LANES), jnp.float32)
    fpar, cpar = parity("flow"), parity("cross")
    for l in range(layers):
        rows[0, l : l + 1, :] = s_ref[l, 0:1, :]
        rows[1, l : l + 1, :] = s_ref[l, length - 1 : length, :]
        rows[2, l : l + 1, :] = film[l // 2, 0:1, :]

    top = lambda a, b, c: jnp.where(fpar == 0, ro_ref[a:b, cut(c)], re_ref[a:b, cut(c)])
    bottom = lambda a, b, c: jnp.where(fpar == 0, re_ref[a:b, cut(c)], ro_ref[a:b, cut(c)])
    nears = []
    for side, halo in ((0, top), (1, bottom)):
        near = [halo(0, layers, c) for c in range(tiles)]
        nears.append(near)
        east = [pltpu.roll(v, 1, 1) for v in near]
        west = [pltpu.roll(v, LANES - 1, 1) for v in near]
        at = 0 if side == 0 else length - SUB
        for c in range(tiles):
            cond = halo(2 * layers, 3 * layers, c)
            rest = halo(3 * layers, 4 * layers, c)
            heat = jnp.where(row == 0, jnp.broadcast_to(rest[chans : chans + 1, :], (SUB, LANES)), 0.0)
            cool = zero
            for k in range(chans):
                cool = jnp.where(row // 2 == k, jnp.broadcast_to(rest[k : k + 1, :], (SUB, LANES)), cool)
            u = near[c]
            lf = jnp.where(lane == 0, zero if c == 0 else east[c - 1], east[c])
            rt = jnp.where(lane == LANES - 1, zero if c == last else west[c + 1], west[c])
            around = (halo(layers, 2 * layers, c) + rows[side, :, cut(c)]) + (lf + rt)
            over = jnp.where(row == 0, u, pltpu.roll(u, 1, 0))
            under = jnp.where(row == SUB - 1, u, pltpu.roll(u, SUB - 1, 0))
            halo_ref[side * layers : (side + 1) * layers, cut(c)] = (
                u
                + cond * (around - 4.0 * u)
                + VERTICAL * ((over - u) + (under - u))
                + rows[2, :, cut(c)] * (cool - u)
                + heat
            )
            spot = 0 if side == 0 else SUB - 1
            for l in range(layers):
                outside = jnp.broadcast_to(u[l : l + 1, :], (SUB, LANES))
                more = jnp.where(row == spot, c_ref[l, at : at + SUB, cut(c)] * outside, 0.0)
                s1_ref[l, at : at + SUB, cut(c)] = s1_in[l, at : at + SUB, cut(c)] + more

    back = LANES - 1
    def fill(right_ref, left_ref):
        for is_left, out in ((0, right_ref), (1, left_ref)):
            base = 0 if is_left else 64
            tile = 0 if is_left else last
            out[0:16, :] = flat_ref[base : base + 16, :]
            t, b = nears[0][tile], nears[1][tile]
            t0 = t if is_left else pltpu.roll(t, 1, 1)
            b1 = pltpu.roll(b, back, 1) if is_left else b
            out[16:24, 0:LANES] = flat_ref[base + 16 : base + 24, 0:LANES] + jnp.where(
                lane == 0, flat_ref[base + 8 : base + 16, 0:LANES] * t0, 0.0
            )
            out[16:24, LANES:] = flat_ref[base + 16 : base + 24, LANES:] + jnp.where(
                lane == back, flat_ref[base + 8 : base + 16, LANES:] * b1, 0.0
            )
            shift = back if is_left else 1
            out[24:32, 0:LANES] = pltpu.roll(t, shift, 1)
            out[24:32, LANES:] = pltpu.roll(b, shift, 1)

    @pl.when(cpar == 0)
    def _():
        fill(even_ref, odd_ref)

    @pl.when(cpar != 0)
    def _():
        fill(odd_ref, even_ref)


def second_step(
    s1_ref, c_ref, w_ref, heat_ref, film, a_ref, halo_ref, s2_ref, kept_ref, base_ref, top, bottom, sums_ref, out_buf, sem
):
    layers, length, width = s1_ref.shape
    chans = w_ref.shape[0]
    tiles = width // LANES
    zero = jnp.zeros((SUB, LANES), jnp.float32)
    for at, out in ((0, top), (1, bottom)):
        for l in range(layers):
            out[l] = jnp.broadcast_to(halo_ref[at * layers + l : at * layers + l + 1, :], (SUB, width))
    sums_ref[...] = jnp.zeros(sums_ref.shape, jnp.float32)

    def layer(l, carry):
        sums = [zero] * tiles

        def load(m, at, c):
            return s1_ref[m, at : at + SUB, cut(c)]

        def emit(r, u, conds, outs, ws):
            at = r * SUB
            for c in range(tiles):
                out_buf[l, at : at + SUB, cut(c)] = outs[c]
                sums[c] = sums[c] + (outs[c] - ws[c])

        stencil(l, load, c_ref, w_ref, film, a_ref, False, top, bottom, emit, length, layers, tiles)
        for c in range(tiles):
            sums_ref[l // 2, :, cut(c)] += sums[c]

        @pl.when(l == 0)
        def _():
            for c in range(tiles):
                total = zero
                for r in range(length // SUB):
                    at = r * SUB
                    heat = heat_ref[at : at + SUB, cut(c)]
                    out_buf[0, at : at + SUB, cut(c)] += heat
                    total = total + heat
                sums_ref[0, :, cut(c)] += total

        @pl.when(l < layers - 2)
        def _():
            pltpu.make_async_copy(out_buf.at[l], s2_ref.at[l], sem.at[l]).start()

        return carry

    lax.fori_loop(0, layers, layer, 0)
    kept_ref[...] = out_buf[layers - 2 :]
    for k in range(chans):
        base_ref[k : k + 1, :] = jnp.sum(sums_ref[k] * film[k], axis=0, keepdims=True)
    for l in range(layers - 2):
        pltpu.make_async_copy(out_buf.at[l], s2_ref.at[l], sem.at[l]).wait()


def add_columns(film, re_ref, ro_ref, ce_ref, co_ref, own_ref, base_ref, total_ref, change_ref):
    layers = SUB
    chans = film.shape[0]
    tiles = base_ref.shape[1] // LANES
    halves = change_ref.shape[1] // LANES
    row, lane = iota(0), iota(1)
    end = LANES - 1
    fpar, cpar = parity("flow"), parity("cross")

    def rolled(v, by):
        return pltpu.roll(v, by, 1)

    sums = []
    for side in range(2):
        spot, tile, base = (0, 0, 0) if side == 0 else (end, tiles - 1, 64)

        def got(a, h, side=side):
            ours, theirs = (co_ref, ce_ref) if side == 0 else (ce_ref, co_ref)
            return jnp.where(cpar == 0, ours[a : a + SUB, cut(h)], theirs[a : a + SUB, cut(h)])

        cond_top = jnp.where(fpar == 0, ro_ref[16:24, cut(tile)], re_ref[16:24, cut(tile)])
        cond_bottom = jnp.where(fpar == 0, re_ref[16:24, cut(tile)], ro_ref[16:24, cut(tile)])
        cond = [own_ref[base + 8 : base + 16, cut(h)] for h in range(halves)]
        first = [cond[h] * got(0, h) for h in range(halves)]
        before, after = cond_top * got(24, 0), cond_bottom * got(24, 1)
        if side == 0:
            after = rolled(after, end)
        else:
            before = rolled(before, 1)
        f = jnp.zeros((SUB, LANES), jnp.float32)
        for k in range(chans):
            f = jnp.where(row // 2 == k, film[k, :, cut(tile)], f)
        keep = (1.0 - 2.0 * VERTICAL) - jnp.broadcast_to(f[:, spot : spot + 1], (SUB, LANES))
        outer_sum = inner_sum = jnp.zeros((SUB, LANES), jnp.float32)
        for h in range(halves):
            d = first[h]
            n = jnp.where(lane == 0, before if h == 0 else rolled(first[h - 1], 1), rolled(d, 1))
            s = jnp.where(lane == end, after if h == halves - 1 else rolled(first[h + 1], end), rolled(d, end))
            beyond = got(16, h) + got(8, h) * own_ref[base : base + 8, cut(h)]
            over = jnp.where(row == 0, d, pltpu.roll(d, 1, 0))
            under = jnp.where(row == SUB - 1, d, pltpu.roll(d, SUB - 1, 0))
            outer = keep * d + cond[h] * (((n + s) + beyond) - 4.0 * d) + VERTICAL * (over + under)
            inner = own_ref[base + 24 : base + 32, cut(h)] * d
            at = 2 * layers * side
            change_ref[at : at + layers, cut(h)] = outer if side == 0 else inner
            change_ref[at + layers : at + 2 * layers, cut(h)] = inner if side == 0 else outer
            outer_sum, inner_sum = outer_sum + outer, inner_sum + inner
        outer_sum = jnp.broadcast_to(jnp.sum(outer_sum, axis=1, keepdims=True), (SUB, LANES))
        inner_sum = jnp.broadcast_to(jnp.sum(inner_sum, axis=1, keepdims=True), (SUB, LANES))
        inner_spot = 1 if side == 0 else end - 1
        both = jnp.where(lane == spot, outer_sum, jnp.where(lane == inner_spot, inner_sum, 0.0))
        sums.append(both + pltpu.roll(both, SUB - 1, 0))
    for k in range(chans):
        for c in range(tiles):
            value = base_ref[k : k + 1, cut(c)]
            if c in (0, tiles - 1):
                value = value + film[k, 0:1, cut(c)] * sums[0 if c == 0 else 1][2 * k : 2 * k + 1, :]
            for j in range(total_ref.shape[0]):
                total_ref[j, 0, k : k + 1, cut(c)] = value


def march(
    length_cells, s_in, w_ref, kept_ref, change_ref, mask_ref, inlet_ref, gain_ref, s2_ref, part_ref, s_buf, w_buf, in_sem, out_sem
):
    chans, length, width = part_ref.shape
    tiles = width // LANES
    row, lane = iota(0), lax.broadcasted_iota(jnp.int32, (length, LANES), 1)
    reads, writes = [], []
    for k in range(chans):
        pair = pl.ds(2 * k, 2)
        reads.append(pltpu.make_async_copy(w_ref.at[k], w_buf.at[k], in_sem.at[1, k]))
        if k < chans - 1:
            reads.append(pltpu.make_async_copy(s_in.at[pair], s_buf.at[pair], in_sem.at[0, k]))
    for copy in reads:
        copy.start()
    s_buf[2 * chans - 2 :] = kept_ref[...]
    i = lax.broadcasted_iota(jnp.int32, (length, length), 0)
    j = lax.broadcasted_iota(jnp.int32, (length, length), 1)
    triangle = jnp.where(j < i, 1.0, jnp.where(j == i, 0.5, 0.0)).astype(jnp.bfloat16)
    middle = jnp.zeros((LANES - 2 * SUB, length), jnp.float32)
    rows = lax.broadcasted_iota(jnp.int32, (SUB, length), 0)
    for k in range(chans):
        for copy in reads[2 * k : 2 * k + 2]:
            copy.wait()
        for l in (2 * k, 2 * k + 1):
            line = lambda n: jnp.broadcast_to(change_ref[n * SUB + l : n * SUB + l + 1, :], (SUB, length))
            first = jnp.where(rows == 0, line(0), jnp.where(rows == 1, line(1), 0.0))
            final = jnp.where(rows == SUB - 2, line(2), jnp.where(rows == SUB - 1, line(3), 0.0))
            turned = jnp.concatenate([first, middle, final], axis=0).T
            s_buf[l, :, cut(0)] += jnp.where(lane < 2, turned, 0.0)
            s_buf[l, :, cut(tiles - 1)] += jnp.where(lane >= LANES - 2, turned, 0.0)
            for side in range(2 if k < chans - 1 else 1):
                view = (l, slice(None), cut(side * (tiles - 1)) if k < chans - 1 else slice(None))
                writes.append(pltpu.make_async_copy(s_buf.at[view], s2_ref.at[view], out_sem.at[side, l]))
                writes[-1].start()
        f = mask_ref[k : k + 1, :].astype(jnp.float32) * FILM
        absorbed = f * ((s_buf[2 * k] + s_buf[2 * k + 1]) - 2.0 * w_buf[k])
        within = None
        for _ in range(3):
            term = absorbed.astype(jnp.bfloat16)
            absorbed = absorbed - term.astype(jnp.float32)
            product = jnp.dot(triangle, term, preferred_element_type=jnp.float32)
            within = product if within is None else within + product
        scale = gain_ref[k : k + 1, :] * (1.0 / length_cells)
        part_ref[k] = inlet_ref[k : k + 1, :] + scale * within
    for copy in writes:
        copy.wait()


def finish(length_cells, part_ref, every_ref, gain_ref, out_ref, buf, sem):
    flow = lax.axis_index("flow")
    total = jnp.zeros(gain_ref.shape, jnp.float32)
    for j in range(every_ref.shape[0]):
        total += jnp.where(j < flow, every_ref[j, 0], 0.0)
    carried = total * gain_ref[...] * (1.0 / length_cells)
    chans = part_ref.shape[0]
    copies = []
    for k in range(chans):
        buf[k] = part_ref[k] + carried[k : k + 1, :]
        copies.append(pltpu.make_async_copy(buf.at[k], out_ref.at[k], sem.at[k]))
        copies[-1].start()
    for copy in copies:
        copy.wait()


def swaps(size):
    even = [(i, i ^ 1) for i in range(size)]
    odd = [(i, i + 1 if i % 2 else i - 1) for i in range(1, size - 1)]
    return even, odd


def f32(*dims):
    return jax.ShapeDtypeStruct(dims, jnp.float32)


def call(kernel, name, out_shape, in_specs, out_specs, scratch, mib, flops, **kw):
    return pl.pallas_call(
        kernel,
        out_shape=out_shape,
        in_specs=in_specs,
        out_specs=out_specs,
        scratch_shapes=scratch,
        compiler_params=pltpu.CompilerParams(vmem_limit_bytes=int(mib * 2**20)),
        cost_estimate=pl.CostEstimate(flops=int(flops), bytes_accessed=0, transcendentals=0),
        name=name,
        **kw,
    )


def shards(s0, cond, cool, index, levels, mask, inlet, gain):
    layers, length, width = s0.shape
    chans = cool.shape[0]
    flows = lax.axis_size("flow")
    count = 4 * layers
    block = f32(layers, length, width)
    buf = lambda *dims: pltpu.VMEM(dims, jnp.float32)
    hbm = lambda *dims: pltpu.HBM(dims, jnp.float32)
    dma = lambda *dims: pltpu.SemaphoreType.DMA(dims)
    in_hbm = lambda x: pltpu.with_memory_space_constraint(x, pltpu.HBM)
    even, odd, film = call(
        edge_rows, "edge_rows", (f32(count, width), f32(count, width), f32(chans, SUB, width)), [HBM] * 6, (VMEM,) * 3,
        [
            buf(2, layers, SUB, width), buf(2, layers, SUB, width), buf(2, chans, SUB, width),
            pltpu.VMEM((2, SUB, width), jnp.int32), pltpu.VMEM(mask.shape, jnp.int32),
            pltpu.SMEM(levels.shape, jnp.float32), dma(2, 4), dma(2),
        ],
        4, 1e5,
    )(*map(in_hbm, (levels, s0, cond, cool, index, mask)))
    even_pairs, odd_pairs = swaps(flows)
    row_odd = lax.ppermute(odd, "flow", odd_pairs)
    row_even = lax.ppermute(even, "flow", even_pairs)

    work = 20 * layers * length * width
    s1, factor, heat, own = call(
        first_step, "first_step", (block, block, f32(length, width), f32(LANES, length)), [SMEM] + [VMEM] * 5, (VMEM,) * 4,
        [], 21, work,
    )(levels, s0, cond, cool, index, film)
    s1, halo, even, odd = call(
        add_rows, "add_rows", (block, f32(2 * layers, width), f32(32, length), f32(32, length)), [VMEM] * 7, (VMEM,) * 4,
        [buf(3, layers, width)], 17, 1e5, input_output_aliases={6: 0},
    )(s0, cond, film, row_even, row_odd, own, s1)
    even_pairs, odd_pairs = swaps(lax.axis_size("cross"))
    col_odd = lax.ppermute(odd, "cross", odd_pairs)
    col_even = lax.ppermute(even, "cross", even_pairs)

    s2, kept, base = call(
        second_step, "second_step", (hbm(layers, length, width), f32(2, length, width), f32(chans, width)), [VMEM] * 7,
        (HBM, VMEM, VMEM),
        [
            buf(layers, SUB, width), buf(layers, SUB, width), buf(chans, SUB, width), buf(layers, length, width),
            dma(layers),
        ],
        23, work,
    )(s1, cond, cool, heat, film, factor, halo)
    totals, change = call(
        add_columns, "add_columns", (f32(flows, 1, chans, width), f32(32, length)), [VMEM] * 7, (VMEM, VMEM), [], 4, 1e4,
    )(film, row_even, row_odd, col_even, col_odd, own, base)
    everyone = lax.all_to_all(totals, "flow", 0, 0, tiled=True)

    cells = float(length * flows)
    s2, part = call(
        functools.partial(march, cells), "march", (hbm(layers, length, width), f32(chans, length, width)),
        [HBM, HBM] + [VMEM] * 5, (HBM, VMEM),
        [buf(layers, length, width), buf(chans, length, width), dma(2, chans), dma(2, layers)],
        14, work // 4, input_output_aliases={0: 0},
    )(in_hbm(s2), in_hbm(cool), kept, change, mask, inlet, gain)
    fluid = call(
        functools.partial(finish, cells), "finish", hbm(chans, length, width), [VMEM] * 3, HBM,
        [buf(chans, length, width), dma(chans)], 6, 1e5,
    )(part, everyone, gain)
    return s2, fluid


def solution(mesh):
    return jax.shard_map(
        shards,
        mesh=mesh,
        in_specs=(
            P(None, "flow", "cross"),
            P(None, "flow", "cross"),
            P(None, "flow", "cross"),
            P("flow", "cross"),
            P(),
            P(None, "cross"),
            P(None, "cross"),
            P(None, "cross"),
        ),
        out_specs=(P(None, "flow", "cross"), P(None, "flow", "cross")),
        check_vma=False,
    )
```

time: 47 us -> 38.9 us (0.83)
  waiting for transfers between devices: 6.68 us -> 3.18 us
  local copies, waits for them, and re-layouts: 3.1 us -> 0.04 us
  starting transfers between devices: 18.4 us -> 16.9 us
    unnamed x20 -> x16, local copies, waits for them, and re-layouts: 3.1 us -> 0.04 us
    all_to_all x1, waiting for transfers between devices: 4.94 us -> 3.16 us  [shards(): everyone = lax.all_to_all(totals, 'flow', 0, 0, tiled=True)]
    ppermute x1, waiting for transfers between devices: 1.73 us -> 0.01 us  [shards(): col_odd = lax.ppermute(odd, 'cross', odd_pairs)]
    all_to_all x1, starting transfers between devices: 7.12 us -> 5.53 us  [shards(): everyone = lax.all_to_all(totals, 'flow', 0, 0, tiled=True)]
    pallas_call x4 -> x5, Pallas kernels: 16.2 us -> 16.1 us  [the longest x1 5.4 us: shards(): call(first_step, 'first_step', (block, block, f32(length, width), f32(LAN...]
  transfers between devices with their start and end apart: 5 -> 5, of which waited for: 2 -> 1; matrix products, arithmetic and copies ran while one was open for 0% -> 0% of each run, Pallas kernels for 15% -> 36%
where the time goes in v2:
time: 38.9 us; the launch traced here: 38.6 us
  Pallas kernels  17.6 us (45%)
  starting transfers between devices  16.9 us (43%)
  waiting for transfers between devices  3.18 us (8%)
  between operations  0.84 us (2%)
    all_to_all x1, starting transfers between devices, shards(): everyone = lax.all_to_all(totals, 'flow', 0, 0, tiled=True)  5.53 us
    pallas_call x1, Pallas kernels, shards(): call(first_step, 'first_step', (block, block, f32(length, width), f32(LAN...  5.4 us
    ppermute x1, starting transfers between devices, shards(): col_odd = lax.ppermute(odd, 'cross', odd_pairs)  5.01 us
    pallas_call x1, Pallas kernels, shards(): call(functools.partial(march, cells), 'march', (hbm(layers, length, width...  4.42 us
    pallas_call x1, Pallas kernels, shards(): call(second_step, 'second_step', (hbm(layers, length, width), f32(2, leng...  3.95 us
    ppermute x1, starting transfers between devices, shards(): row_odd = lax.ppermute(odd, 'flow', odd_pairs)  3.91 us
    all_to_all x1, waiting for transfers between devices, shards(): everyone = lax.all_to_all(totals, 'flow', 0, 0, tiled=True)  3.16 us
    ppermute x1, starting transfers between devices, shards(): col_even = lax.ppermute(even, 'cross', even_pairs)  1.72 us
  transfers between devices with their start and end apart: 5, of which 1 were waited for; matrix products, arithmetic and copies ran while one was open for 0% of the time, Pallas kernels for 36%

profile of v2, /device:TPU:3, one launch (start us, length us, event | category | flops | bytes accessed | tf_op | source)
XLA Modules:
  0.0 38.6 jit_solution(17823369773948176689)
XLA Ops:
  0.6 0.0 copy-start.2
  0.6 0.0 copy-start
  0.7 0.0 copy-start.1
  0.7 0.0 copy-start.7
  0.7 0.0 copy-start.3
  0.7 1.4 %edge_rows.1 = (f32[32,512]{1,0:T(8,128)S(1)}, f32[32,512]{1,0:T(8,128)S(1)}, f32[4,8,512]{2,1,0:T(8,128)S(1)}) custom-call(f32[16]{0:T(128)} %levels_ref.3, f32[8,256,512]{2,1,0:T(8,128)} %s_ref.5, f32[8,256,512]{2,1,0:T(8,128)} %c_ref.7, f32[4,256,512]{2,1,0:T(8,128)} %w_ref.7, s32[256,512]{1,0:T(8,128)} %p_ref.3, s32[4,512]{1,0:T(4,128)} %mask_ref.3), custom_call_target="tpu_custom_call" | custom-call | flops 100000 | tf_op jit(solution)/shard_map/edge_rows/pallas_call | solution.py:469
  2.1 0.8 %collective-permute-start = (f32[32,512]{1,0:T(8,128)S(1)}, f32[32,512]{1,0:T(8,128)S(1)}, u32[]{:S(2)}, u32[]{:S(2)}) collective-permute-start(f32[32,512]{1,0:T(8,128)S(1)} %get-tuple-element.21), channel_id=1, source_target_pairs={{0,8},{8,0},{16,24},{24,16},{32,40},{40,32},{48,56},{56,48},{64,72... | collective-permute-start | bytes 196616 | tf_op jit(solution)/shard_map/ppermute | solution.py:480
  2.9 3.9 %collective-permute-start.1 = (f32[32,512]{1,0:T(8,128)S(1)}, f32[32,512]{1,0:T(8,128)S(1)}, u32[]{:S(2)}, u32[]{:S(2)}) collective-permute-start(f32[32,512]{1,0:T(8,128)S(1)} %get-tuple-element.22), channel_id=1, source_target_pairs={{8,16},{16,8},{24,32},{32,24},{40,48},{48,40},{56,64},{64,56},{72,... | collective-permute-start | bytes 196616 | tf_op jit(solution)/shard_map/ppermute | solution.py:479
  6.8 0.0 copy-done.2
  6.8 0.0 copy-done
  6.8 0.0 copy-done.1
  6.8 0.0 copy-done.7
  6.9 0.0 copy-done.3
  6.9 5.4 %first_step.1 = (f32[8,256,512]{2,1,0:T(8,128)S(1)}, f32[8,256,512]{2,1,0:T(8,128)S(1)}, f32[256,512]{1,0:T(8,128)S(1)}, f32[128,256]{1,0:T(8,128)S(1)}) custom-call(f32[16]{0:T(128)S(1)} %copy-done.7, f32[8,256,512]{2,1,0:T(8,128)S(1)} %copy-done.1, f32[8,256,512]{2,1,0:T(8,128)S(1)} %copy-done, f32[4,256,512]{2,1,0:T(8,128)S(1)} %copy-done.2, ...), custom_call_target="tpu_custom_call" | custom-call | flops 20971520 | tf_op jit(solution)/shard_map/first_step/pallas_call | solution.py:483
  12.3 0.0 collective-permute-done.re_ref
  12.3 0.0 collective-permute-done.1.ro_ref
  12.3 0.2 add_rows.1
  12.5 1.7 %collective-permute-start.2 = (f32[32,256]{1,0:T(8,128)S(1)}, f32[32,256]{1,0:T(8,128)S(1)}, u32[]{:S(2)}, u32[]{:S(2)}) collective-permute-start(f32[32,256]{1,0:T(8,128)S(1)} %get-tuple-element.31), channel_id=1, source_target_pairs={{0,1},{1,0},{2,3},{3,2},{4,5},{5,4},{6,7},{7,6},{8,9},{9,8},{10,11... | collective-permute-start | bytes 98312 | tf_op jit(solution)/shard_map/ppermute | solution.py:493
  14.2 5.0 %collective-permute-start.3 = (f32[32,256]{1,0:T(8,128)S(1)}, f32[32,256]{1,0:T(8,128)S(1)}, u32[]{:S(2)}, u32[]{:S(2)}) collective-permute-start(f32[32,256]{1,0:T(8,128)S(1)} %get-tuple-element.32), channel_id=1, source_target_pairs={{1,2},{2,1},{3,4},{4,3},{5,6},{6,5},{9,10},{10,9},{11,12},{12,11},... | collective-permute-start | bytes 98312 | tf_op jit(solution)/shard_map/ppermute | solution.py:492
  19.2 0.0 copy-start.4
  19.2 0.0 copy-start.5
  19.2 0.0 copy-start.6
  19.2 3.9 %second_step.1 = (f32[8,256,512]{2,1,0:T(8,128)}, f32[2,256,512]{2,1,0:T(8,128)S(1)}, f32[4,512]{1,0:T(4,128)S(1)}) custom-call(f32[8,256,512]{2,1,0:T(8,128)S(1)} %get-tuple-element.25.s1_ref, f32[8,256,512]{2,1,0:T(8,128)S(1)} %copy-done, f32[4,256,512]{2,1,0:T(8,128)S(1)} %copy-done.2, f32[256,512]{1,0:T(8,128)S(1)} %get-tuple-element.26.heat_ref, ...), custom_call_target="tpu_custom_call" | custom-call | flops 20971520 | tf_op jit(solution)/shard_map/second_step/pallas_call | solution.py:495
  23.2 0.0 collective-permute-done.2.ce_ref
  23.2 0.0 collective-permute-done.3.co_ref
  23.2 0.9 %add_columns.1 = (f32[16,1,4,512]{3,2,1,0:T(4,128)}, f32[32,256]{1,0:T(8,128)S(1)}) custom-call(f32[4,8,512]{2,1,0:T(8,128)S(1)} %get-tuple-element.20.film, f32[32,512]{1,0:T(8,128)S(1)} %collective-permute-done.re_ref, f32[32,512]{1,0:T(8,128)S(1)} %collective-permute-done.1.ro_ref, f32[32,256]{1,0:T(8,128)S(1)} %collective-permute-done.2.ce_ref, ...), custom_call_target="tpu_custom_call" | custom-call | flops 10000 | tf_op jit(solution)/shard_map/add_columns/pallas_call | solution.py:504
  24.1 5.5 %all-to-all-start = ((f32[16,1,4,512]{3,2,1,0:T(4,128)}), f32[16,1,4,512]{3,2,1,0:T(4,128)S(1)}, u32[]{:S(2)}, u32[]{:S(2)}) async-start(f32[16,1,4,512]{3,2,1,0:T(4,128)} %get-tuple-element.37), calls=%async_computation | async-start | bytes 262144 | tf_op jit(solution)/shard_map/all_to_all | solution.py:507
  29.6 0.0 copy-done.4
  29.6 0.0 copy-done.5
  29.6 0.0 copy-done.6
  29.6 4.4 %march.1 = (f32[8,256,512]{2,1,0:T(8,128)}, f32[4,256,512]{2,1,0:T(8,128)S(1)}) custom-call(f32[8,256,512]{2,1,0:T(8,128)} %get-tuple-element.29.s_in, f32[4,256,512]{2,1,0:T(8,128)} %w_ref.7, f32[2,256,512]{2,1,0:T(8,128)S(1)} %get-tuple-element.30.kept_ref, f32[32,256]{1,0:T(8,128)S(1)} %get-tuple-element.34.change_ref, ...), custom_call_target="tpu_custom_call", output_to_operand_aliasing={{0}: (0, {})} | custom-call | flops 5242880 | tf_op jit(solution)/shard_map/march/pallas_call | solution.py:510
  34.1 3.2 %all-to-all-done.every_ref = f32[16,1,4,512]{3,2,1,0:T(4,128)S(1)} async-done(((f32[16,1,4,512]{3,2,1,0:T(4,128)}), f32[16,1,4,512]{3,2,1,0:T(4,128)S(1)}, u32[]{:S(2)}, u32[]{:S(2)}) %all-to-all-start) | async-done | bytes 131104 | tf_op jit(solution)/shard_map/all_to_all | solution.py:507
  37.2 1.4 %finish.1 = f32[4,256,512]{2,1,0:T(8,128)} custom-call(f32[4,256,512]{2,1,0:T(8,128)S(1)} %get-tuple-element.36.part_ref, f32[16,1,4,512]{3,2,1,0:T(4,128)S(1)} %all-to-all-done.every_ref, f32[4,512]{1,0:T(4,128)S(1)} %copy-done.5), custom_call_target="tpu_custom_call" | custom-call | flops 100000 | tf_op jit(solution)/shard_map/finish/pallas_call | solution.py:516
Async XLA Ops:
  0.6 6.2 %copy-start.2 = (f32[4,256,512]{2,1,0:T(8,128)S(1)}, f32[4,256,512]{2,1,0:T(8,128)}, u32[]{:S(2)}) copy-start(f32[4,256,512]{2,1,0:T(8,128)} %w_ref.7) | copy-start | bytes 6291460
  0.6 6.2 %copy-start = (f32[8,256,512]{2,1,0:T(8,128)S(1)}, f32[8,256,512]{2,1,0:T(8,128)}, u32[]{:S(2)}) copy-start(f32[8,256,512]{2,1,0:T(8,128)} %c_ref.7) | copy-start | bytes 12582916
  0.7 6.2 %copy-start.1 = (f32[8,256,512]{2,1,0:T(8,128)S(1)}, f32[8,256,512]{2,1,0:T(8,128)}, u32[]{:S(2)}) copy-start(f32[8,256,512]{2,1,0:T(8,128)} %s_ref.5) | copy-start | bytes 12582916
  0.7 6.2 %copy-start.7 = (f32[16]{0:T(128)S(1)}, f32[16]{0:T(128)}, u32[]{:S(2)}) copy-start(f32[16]{0:T(128)} %levels_ref.3) | copy-start | bytes 196
  0.7 6.2 %copy-start.3 = (s32[256,512]{1,0:T(8,128)S(1)}, s32[256,512]{1,0:T(8,128)}, u32[]{:S(2)}) copy-start(s32[256,512]{1,0:T(8,128)} %p_ref.3) | copy-start | bytes 1572868
  2.1 10.1 %collective-permute-start = (f32[32,512]{1,0:T(8,128)S(1)}, f32[32,512]{1,0:T(8,128)S(1)}, u32[]{:S(2)}, u32[]{:S(2)}) collective-permute-start(f32[32,512]{1,0:T(8,128)S(1)} %get-tuple-element.21), channel_id=1, source_target_pairs={{0,8},{8,0},{16,24},{24,16},{32,40},{40,32},{48,56},{56,48},{64,72... | collective-permute-start | bytes 196616 | tf_op jit(solution)/shard_map/ppermute | solution.py:480
  2.9 9.4 %collective-permute-start.1 = (f32[32,512]{1,0:T(8,128)S(1)}, f32[32,512]{1,0:T(8,128)S(1)}, u32[]{:S(2)}, u32[]{:S(2)}) collective-permute-start(f32[32,512]{1,0:T(8,128)S(1)} %get-tuple-element.22), channel_id=1, source_target_pairs={{8,16},{16,8},{24,32},{32,24},{40,48},{48,40},{56,64},{64,56},{72,... | collective-permute-start | bytes 196616 | tf_op jit(solution)/shard_map/ppermute | solution.py:479
  12.5 10.7 %collective-permute-start.2 = (f32[32,256]{1,0:T(8,128)S(1)}, f32[32,256]{1,0:T(8,128)S(1)}, u32[]{:S(2)}, u32[]{:S(2)}) collective-permute-start(f32[32,256]{1,0:T(8,128)S(1)} %get-tuple-element.31), channel_id=1, source_target_pairs={{0,1},{1,0},{2,3},{3,2},{4,5},{5,4},{6,7},{7,6},{8,9},{9,8},{10,11... | collective-permute-start | bytes 98312 | tf_op jit(solution)/shard_map/ppermute | solution.py:493
  14.2 9.0 %collective-permute-start.3 = (f32[32,256]{1,0:T(8,128)S(1)}, f32[32,256]{1,0:T(8,128)S(1)}, u32[]{:S(2)}, u32[]{:S(2)}) collective-permute-start(f32[32,256]{1,0:T(8,128)S(1)} %get-tuple-element.32), channel_id=1, source_target_pairs={{1,2},{2,1},{3,4},{4,3},{5,6},{6,5},{9,10},{10,9},{11,12},{12,11},... | collective-permute-start | bytes 98312 | tf_op jit(solution)/shard_map/ppermute | solution.py:492
  19.2 10.4 %copy-start.4 = (s32[4,512]{1,0:T(4,128)S(1)}, s32[4,512]{1,0:T(4,128)}, u32[]{:S(2)}) copy-start(s32[4,512]{1,0:T(4,128)} %mask_ref.3) | copy-start | bytes 24580
  19.2 10.4 %copy-start.5 = (f32[4,512]{1,0:T(4,128)S(1)}, f32[4,512]{1,0:T(4,128)}, u32[]{:S(2)}) copy-start(f32[4,512]{1,0:T(4,128)} %gain_ref.3) | copy-start | bytes 24580
  19.2 10.4 %copy-start.6 = (f32[4,512]{1,0:T(4,128)S(1)}, f32[4,512]{1,0:T(4,128)}, u32[]{:S(2)}) copy-start(f32[4,512]{1,0:T(4,128)} %inlet_ref.1) | copy-start | bytes 24580
  24.1 13.1 %all-to-all-start = ((f32[16,1,4,512]{3,2,1,0:T(4,128)}), f32[16,1,4,512]{3,2,1,0:T(4,128)S(1)}, u32[]{:S(2)}, u32[]{:S(2)}) async-start(f32[16,1,4,512]{3,2,1,0:T(4,128)} %get-tuple-element.37), calls=%async_computation | async-start | bytes 262144 | tf_op jit(solution)/shard_map/all_to_all | solution.py:507
